TPU v7x, 8 devices: a whole 2x2x1 slice. The times are simulated.
8 devices in a mesh: dp: 1 (over z), etp: 2 (over y), ep: 4 (over x, core).
Axes of the slice: x: 2, y: 2, z: 1, core: 2. Of those that a mesh axis runs over, the one named last changes fastest.
Arguments:
- u_rows: bfloat16 [512, 1536], P(('dp', 'ep', 'etp'))
- dy_rows: bfloat16 [512, 1536], P(('dp', 'ep', 'etp'))
- topk_ids: int32 [512, 8], P(('dp', 'ep', 'etp'))
- w_router: bfloat16 [1536, 40], replicated
- w_gate: bfloat16 [40, 1536, 512], P('ep', None, 'etp')
- w_up: bfloat16 [40, 1536, 512], P('ep', None, 'etp')
- w_down: bfloat16 [40, 512, 1536], P('ep', 'etp')
Outputs:
- output 1: bfloat16 [512, 1536], P(('dp', 'ep', 'etp'))
- output 2: bfloat16 [512, 1536], P(('dp', 'ep', 'etp'))
- output 3: float32 [40, 1536, 512], P(('dp', 'ep'), None, 'etp')
- output 4: float32 [40, 1536, 512], P(('dp', 'ep'), None, 'etp')
- output 5: float32 [40, 512, 1536], P(('dp', 'ep'), 'etp')
- output 6: float32 [1536, 40], P('dp')
All inputs are finite; a program needn't handle non-finite values.
Results may differ from a plain program's by a relative error of at most 0.010856.
Values are sent between devices in bfloat16 or wider.
A program may use at most 1 GiB of HBM per device.

v0:
```python
import jax
import jax.numpy as jnp
from jax import lax
from jax.sharding import PartitionSpec as P


def row_bound(tok_dev, top_k, experts):
    return min(tok_dev, (4 * tok_dev * top_k + experts - 1) // experts)


def slot_layout(expert_ids, experts, slot_count):
    tokens, top_k = expert_ids.shape
    flat_ids = expert_ids.reshape(-1)
    one_hot = (flat_ids[:, None] == jnp.arange(experts, dtype=jnp.int32)[None, :]).astype(jnp.int32)
    pair_rank = jnp.sum((jnp.cumsum(one_hot, axis=0) - one_hot) * one_hot, axis=1)
    pair_slot = flat_ids * slot_count + pair_rank
    slot_pair = jnp.full((experts * slot_count,), tokens * top_k, jnp.int32).at[pair_slot].set(jnp.arange(tokens * top_k, dtype=jnp.int32))
    return pair_slot.reshape(tokens, top_k), slot_pair


def solution(mesh):
    ep_size = mesh.shape["ep"]
    etp_size = mesh.shape["etp"]
    tok_spec = P(("dp", "ep", "etp"), None)
    col_spec = P("ep", None, "etp")
    row_spec = P("ep", "etp", None)
    in_specs = (tok_spec, tok_spec, tok_spec, P(None, None), col_spec, col_spec, row_spec)
    out_specs = (tok_spec, tok_spec, P(("dp", "ep"), None, "etp"), P(("dp", "ep"), None, "etp"), P(("dp", "ep"), "etp", None), P("dp", None))

    def device_step(u_loc, dy_loc, ids_loc, w_router, w_gate, w_up, w_down):
        tok_dev, d_model = u_loc.shape
        top_k = ids_loc.shape[1]
        experts = w_router.shape[1]
        local_exp = w_gate.shape[0]
        cap_slots = etp_size * row_bound(tok_dev, top_k, experts)
        logits = jnp.dot(u_loc, w_router, preferred_element_type=jnp.float32)
        router_prob = jax.nn.softmax(logits, axis=-1)
        gate_loc = jnp.take_along_axis(router_prob, ids_loc, axis=1)
        u_grp = lax.all_gather(u_loc, "etp", axis=0, tiled=True)
        ids_grp = lax.all_gather(ids_loc, "etp", axis=0, tiled=True)
        gate_grp = lax.all_gather(gate_loc, "etp", axis=0, tiled=True)
        pair_slot, slot_pair = slot_layout(ids_grp, experts, cap_slots)
        slot_tok = slot_pair // top_k
        x_send = jnp.take(u_grp, slot_tok, axis=0, mode="fill", fill_value=0)
        x_recv = lax.all_to_all(x_send.reshape(experts, cap_slots, d_model), "ep", 0, 0, tiled=True).reshape(ep_size, local_exp, cap_slots, d_model)
        h_gate = jnp.einsum("secd,edf->secf", x_recv, w_gate, preferred_element_type=jnp.float32).astype(jnp.bfloat16)
        h_up = jnp.einsum("secd,edf->secf", x_recv, w_up, preferred_element_type=jnp.float32).astype(jnp.bfloat16)
        gate_f32 = h_gate.astype(jnp.float32)
        up_f32 = h_up.astype(jnp.float32)
        sig_gate = jax.nn.sigmoid(gate_f32)
        silu_gate = gate_f32 * sig_gate
        act_rows = (silu_gate * up_f32).astype(jnp.bfloat16)
        out_part = jnp.einsum("secf,efd->secd", act_rows, w_down, preferred_element_type=jnp.float32).astype(jnp.bfloat16)
        out_back = lax.all_to_all(out_part.reshape(experts, cap_slots, d_model), "ep", 0, 0, tiled=True)
        out_pairs = jnp.take(out_back.reshape(experts * cap_slots, d_model), pair_slot, axis=0)
        moe_part = jnp.einsum("tk,tkd->td", gate_grp, out_pairs, preferred_element_type=jnp.float32)
        moe_own = lax.psum_scatter(moe_part, "etp", scatter_dimension=0, tiled=True)
        y_loc = (u_loc.astype(jnp.float32) + moe_own).astype(jnp.bfloat16)

        dy_grp = lax.all_gather(dy_loc, "etp", axis=0, tiled=True)
        dgate_part = jnp.einsum("td,tkd->tk", dy_grp, out_pairs, preferred_element_type=jnp.float32)
        dgate_loc = lax.psum_scatter(dgate_part, "etp", scatter_dimension=0, tiled=True)
        slot_gate = jnp.take(gate_grp.reshape(-1), slot_pair, mode="fill", fill_value=0.0)
        cot_slots = jnp.take(dy_grp, slot_tok, axis=0, mode="fill", fill_value=0)
        do_send = (cot_slots.astype(jnp.float32) * slot_gate[:, None]).astype(jnp.bfloat16)
        do_recv = lax.all_to_all(do_send.reshape(experts, cap_slots, d_model), "ep", 0, 0, tiled=True).reshape(ep_size, local_exp, cap_slots, d_model)
        dw_down = jnp.einsum("secf,secd->efd", act_rows, do_recv, preferred_element_type=jnp.float32)
        d_act = jnp.einsum("secd,efd->secf", do_recv, w_down, preferred_element_type=jnp.float32).astype(jnp.bfloat16).astype(jnp.float32)
        d_gate_h = (d_act * up_f32 * sig_gate * (1.0 + gate_f32 * (1.0 - sig_gate))).astype(jnp.bfloat16)
        d_up_h = (d_act * silu_gate).astype(jnp.bfloat16)
        dw_gate = jnp.einsum("secd,secf->edf", x_recv, d_gate_h, preferred_element_type=jnp.float32)
        dw_up = jnp.einsum("secd,secf->edf", x_recv, d_up_h, preferred_element_type=jnp.float32)
        dx_part = (jnp.einsum("secf,edf->secd", d_gate_h, w_gate, preferred_element_type=jnp.float32) + jnp.einsum("secf,edf->secd", d_up_h, w_up, preferred_element_type=jnp.float32)).astype(jnp.bfloat16)
        dx_back = lax.all_to_all(dx_part.reshape(experts, cap_slots, d_model), "ep", 0, 0, tiled=True)
        dx_pairs = jnp.take(dx_back.reshape(experts * cap_slots, d_model), pair_slot, axis=0)
        du_part = jnp.sum(dx_pairs, axis=1, dtype=jnp.float32)
        du_moe = lax.psum_scatter(du_part, "etp", scatter_dimension=0, tiled=True)
        expert_hot = (ids_loc[:, :, None] == jnp.arange(experts, dtype=jnp.int32)[None, None, :]).astype(jnp.float32)
        d_prob = jnp.einsum("tk,tke->te", dgate_loc, expert_hot)
        d_logit = router_prob * (d_prob - jnp.sum(router_prob * d_prob, axis=-1, keepdims=True))
        dw_router = lax.psum(jnp.einsum("td,te->de", u_loc, d_logit, preferred_element_type=jnp.float32), ("etp", "ep"))
        du_router = jnp.einsum("te,de->td", d_logit, w_router, preferred_element_type=jnp.float32)
        du_loc = (dy_loc.astype(jnp.float32) + du_moe + du_router).astype(jnp.bfloat16)
        return y_loc, du_loc, dw_gate, dw_up, dw_down, dw_router

    return jax.shard_map(device_step, mesh=mesh, in_specs=in_specs, out_specs=out_specs, check_vma=False)
```

profile of v0, /device:TPU:0, one launch (start us, length us, event | category | flops | bytes accessed | tf_op | source)
XLA Modules:
  0.0 897.4 jit_solution(1845857471963508027)
XLA Ops:
  19.9 11.3 %reduce-window.6 = s32[40,8,128]{2,1,0:T(8,128)S(1)} reduce-window(s32[40,8,128]{2,1,0:T(8,128)S(1)} %fusion.56, s32[]{:T(128)} %constant.52.clone.1), window={size=1x1x128 pad=0_0x0_0x127_0}, to_apply=%region_2.0 | reduce-window | flops 5201920 | bytes 327684 | tf_op jit(solution)/shard_map/reduce-window
  36.2 15.0 %gather_fusion.2 = bf16[4160,1536]{1,0:T(8,128)(2,1)} fusion(bf16[128,1536]{1,0:T(8,128)(2,1)S(1)} %all_gather.13, s32[5120]{0:T(1024)S(1)} %pad_clamp_fusion.1), kind=kCustom, calls=%fused_computation.clone | custom fusion | bytes 25575680 | tf_op jit(solution)/shard_map/jit(_take)/gather | solution.py:44
  58.2 144.5 %all_to_all.20 = bf16[40,104,1536]{2,1,0:T(8,128)(2,1)} all-to-all(bf16[40,104,1536]{2,1,0:T(8,128)(2,1)S(1)} %bitcast.166), channel_id=1, replica_groups=mesh['dp'=1,'etp'=2,'ep'=4] {'ep'}, dimensions={0} | all-to-all | bytes 25559040 | tf_op jit(solution)/shard_map/all_to_all | solution.py:45
  202.6 11.7 %fusion.39 = bf16[10,4,104,256]{3,2,1,0:T(8,128)(2,1)} fusion(bf16[10,1536,256]{2,1,0:T(8,128)(2,1)} %param.16, bf16[4,10,104,1536]{3,2,1,0:T(8,128)(2,1)} %bitcast.159), kind=kOutput, calls=%fused_computation.57 | convolution fusion | flops 3272622080 | bytes 22773760 | tf_op jit(solution)/shard_map/secd,edf->secf/dot_general | solution.py:47
  214.3 11.7 %fusion.34 = bf16[10,4,104,256]{3,2,1,0:T(8,128)(2,1)} fusion(bf16[10,1536,256]{2,1,0:T(8,128)(2,1)} %param.15, bf16[4,10,104,1536]{3,2,1,0:T(8,128)(2,1)} %bitcast.160), kind=kOutput, calls=%fused_computation.56 | convolution fusion | flops 3272622080 | bytes 22773760 | tf_op jit(solution)/shard_map/secd,edf->secf/dot_general | solution.py:46
  226.0 12.9 %fusion.8 = bf16[4,10,104,1536]{3,2,0,1:T(8,128)(2,1)} fusion(bf16[10,256,1536]{2,1,0:T(8,128)(2,1)} %param.17, bf16[10,4,104,256]{3,2,1,0:T(8,128)(2,1)} %fusion.39, bf16[10,4,104,256]{3,2,1,0:T(8,128)(2,1)} %fusion.34), kind=kOutput, calls=%fused_computation.19 | convolution fusion | flops 3286466560 | bytes 24903680 | tf_op jit(solution)/shard_map/secf,efd->secd/dot_general | solution.py:53
  238.9 10.8 %copy.81 = bf16[4,10,104,1536]{3,2,1,0:T(8,128)(2,1)} copy(bf16[4,10,104,1536]{3,2,0,1:T(8,128)(2,1)} %fusion.8) | data formatting | bytes 25559040 | tf_op jit(solution)/shard_map/convert_element_type | solution.py:53
  256.9 8.6 all_gather.15
  265.7 130.4 %all-to-all-done.1 = bf16[40,104,1536]{2,1,0:T(8,128)(2,1)} async-done(((bf16[40,104,1536]{2,1,0:T(8,128)(2,1)}), bf16[40,104,1536]{2,1,0:T(8,128)(2,1)}, u32[]{:S(2)}, u32[]{:S(2)}) %all-to-all-start.1) | async-done | bytes 12779552 | tf_op jit(solution)/shard_map/all_to_all | solution.py:54
  396.1 13.5 %gather_fusion.3 = bf16[1024,1536]{1,0:T(8,128)(2,1)} fusion(bf16[4160,1536]{1,0:T(8,128)(2,1)} %bitcast.20, s32[1024]{0:T(1024)S(1)} %broadcast_clamp_fusion), kind=kCustom, calls=%fused_computation.1.clone | custom fusion | bytes 6295552 | tf_op jit(solution)/shard_map/jit(_take)/gather | solution.py:55
  414.7 14.9 %gather_fusion.4 = bf16[4160,1536]{1,0:T(8,128)(2,1)} fusion(bf16[128,1536]{1,0:T(8,128)(2,1)S(1)} %all_gather.15, s32[5120]{0:T(1024)S(1)} %pad_clamp_fusion.1), kind=kCustom, calls=%fused_computation.2.clone | custom fusion | bytes 25575680 | tf_op jit(solution)/shard_map/jit(_take)/gather | solution.py:64
  439.6 15.0 %gather_fusion = f32[4160]{0:T(1024)S(1)} fusion(f32[1024]{0:T(1024)S(1)} %reshape.123, s32[5120]{0:T(1024)S(1)} %pad_clamp_fusion), kind=kCustom, calls=%fused_computation.4 | custom fusion | bytes 49920 | tf_op jit(solution)/shard_map/jit(_take)/gather | solution.py:63
  454.6 7.8 multiply_convert_fusion
  462.4 144.3 %all_to_all.21 = bf16[40,104,1536]{2,1,0:T(8,128)(2,1)} all-to-all(bf16[40,104,1536]{2,1,0:T(8,128)(2,1)S(1)} %bitcast.165), channel_id=1, replica_groups=mesh['dp'=1,'etp'=2,'ep'=4] {'ep'}, dimensions={0} | all-to-all | bytes 25559040 | tf_op jit(solution)/shard_map/all_to_all | solution.py:66
  606.7 12.7 %fusion.23 = (bf16[4,10,104,256]{3,2,0,1:T(8,128)(2,1)}, bf16[4,10,104,256]{3,2,0,1:T(8,128)(2,1)S(1)}) fusion(bf16[10,4,104,256]{3,2,1,0:T(8,128)(2,1)} %fusion.34, bf16[10,4,104,256]{3,2,1,0:T(8,128)(2,1)} %fusion.39, bf16[10,256,1536]{2,1,0:T(8,128)(2,1)} %param.17, bf16[4,10,104,1536]{3,2,1,0:T(8,128)(2,1)} %bitcast.167), kind=kOutput, calls=%fused_computation.37 | convolution fusion | flops 3289661440 | bytes 29163520 | tf_op jit(solution)/shard_map/secd,efd->secf/dot_general | solution.py:68
  619.3 14.3 %fusion.12 = f32[10,4,104,1536]{3,2,1,0:T(8,128)} fusion(bf16[4,10,104,256]{3,2,0,1:T(8,128)(2,1)S(1)} %get-tuple-element.15, bf16[10,1536,256]{2,1,0:T(8,128)(2,1)} %param.15), kind=kOutput, calls=%fused_computation.23 | convolution fusion | flops 3271557120 | bytes 35553280 | tf_op jit(solution)/shard_map/secf,edf->secd/dot_general | solution.py:73
  633.7 17.6 %fusion.9 = bf16[4,10,104,1536]{3,2,0,1:T(8,128)(2,1)} fusion(f32[10,4,104,1536]{3,2,1,0:T(8,128)} %fusion.12, bf16[4,10,104,256]{3,2,0,1:T(8,128)(2,1)} %get-tuple-element.14, bf16[10,1536,256]{2,1,0:T(8,128)(2,1)} %param.16), kind=kOutput, calls=%fused_computation.20 | convolution fusion | flops 3284336640 | bytes 48332800 | tf_op jit(solution)/shard_map/secf,edf->secd/dot_general | solution.py:73
  651.3 10.8 %copy.86 = bf16[4,10,104,1536]{3,2,1,0:T(8,128)(2,1)} copy(bf16[4,10,104,1536]{3,2,0,1:T(8,128)(2,1)} %fusion.9) | data formatting | bytes 25559040 | tf_op jit(solution)/shard_map/convert_element_type | solution.py:73
  672.7 135.6 %all-to-all-done.3 = bf16[40,104,1536]{2,1,0:T(8,128)(2,1)} async-done(((bf16[40,104,1536]{2,1,0:T(8,128)(2,1)}), bf16[40,104,1536]{2,1,0:T(8,128)(2,1)}, u32[]{:S(2)}, u32[]{:S(2)}) %all-to-all-start.3) | async-done | bytes 12779552 | tf_op jit(solution)/shard_map/all_to_all | solution.py:74
  808.3 13.5 %gather_fusion.5 = bf16[1024,1536]{1,0:T(8,128)(2,1)} fusion(bf16[4160,1536]{1,0:T(8,128)(2,1)} %bitcast.31, s32[1024]{0:T(1024)S(1)} %broadcast_clamp_fusion), kind=kCustom, calls=%fused_computation.3.clone | custom fusion | bytes 6295552 | tf_op jit(solution)/shard_map/jit(_take)/gather | solution.py:75
  830.5 11.7 %convolution_bitcast_fusion.1 = f32[10,1536,256]{2,1,0:T(8,128)} fusion(bf16[4,10,104,1536]{3,2,1,0:T(8,128)(2,1)} %bitcast.161, bf16[4,10,104,256]{3,2,0,1:T(8,128)(2,1)S(1)} %get-tuple-element.15), kind=kOutput, calls=%fused_computation.30 | convolution fusion | flops 3271557120 | bytes 30638080 | tf_op jit(solution)/shard_map/secd,secf->edf/dot_general | solution.py:71
  842.3 11.7 %convolution_bitcast_fusion = f32[10,1536,256]{2,1,0:T(8,128)} fusion(bf16[4,10,104,1536]{3,2,1,0:T(8,128)(2,1)} %bitcast.162, bf16[4,10,104,256]{3,2,0,1:T(8,128)(2,1)S(1)} %copy-done.1), kind=kOutput, calls=%fused_computation.29 | convolution fusion | flops 3271557120 | bytes 30638080 | tf_op jit(solution)/shard_map/secd,secf->edf/dot_general | solution.py:72
  854.0 15.5 %fusion.17 = f32[10,256,1536]{2,1,0:T(8,128)} fusion(bf16[4,10,104,1536]{3,2,1,0:T(8,128)(2,1)} %bitcast.168, bf16[10,4,104,256]{3,2,1,0:T(8,128)(2,1)S(1)} %copy-done.7, bf16[10,4,104,256]{3,2,1,0:T(8,128)(2,1)} %fusion.34), kind=kOutput, calls=%fused_computation.28 | convolution fusion | flops 3280076800 | bytes 32768000 | tf_op jit(solution)/shard_map/secf,secd->efd/dot_general | solution.py:67
  871.5 17.4 %all-reduce.2.cloned.1.call-done = f32[1536,40]{0,1:T(8,128)} async-done(((f32[1536,40]{0,1:T(8,128)}), f32[1536,40]{0,1:T(8,128)}) %all-reduce.2.cloned.1.call-update) | async-done | bytes 245776 | tf_op jit(solution)/shard_map/psum | solution.py:81
  (87 shorter events, 69.7 us)
Async XLA Ops:
  7.2 258.3 %copy-start = (bf16[1536,40]{0,1:T(8,128)(2,1)S(1)}, bf16[1536,40]{0,1:T(8,128)(2,1)}, u32[]{:S(2)}) copy-start(bf16[1536,40]{0,1:T(8,128)(2,1)} %param.14) | copy-start | bytes 368644
  249.7 7.1 copy-start.4
  249.7 15.7 %copy-start.2 = (bf16[64,1536]{1,0:T(8,128)(2,1)S(1)}, bf16[64,1536]{1,0:T(8,128)(2,1)}, u32[]{:S(2)}) copy-start(bf16[64,1536]{1,0:T(8,128)(2,1)} %param.11) | copy-start | bytes 589828
  249.7 16.0 %copy-start.6 = (s32[64,8]{0,1:T(8,128)S(1)}, s32[64,8]{0,1:T(8,128)}, u32[]{:S(2)}) copy-start(s32[64,8]{0,1:T(8,128)} %param.13) | copy-start | bytes 6148
  249.7 146.4 %all-to-all-start.1 = ((bf16[40,104,1536]{2,1,0:T(8,128)(2,1)}), bf16[40,104,1536]{2,1,0:T(8,128)(2,1)}, u32[]{:S(2)}, u32[]{:S(2)}) async-start(bf16[40,104,1536]{2,1,0:T(8,128)(2,1)} %bitcast.163), calls=%async_computation.1 | async-start | bytes 25559040 | tf_op jit(solution)/shard_map/all_to_all | solution.py:54
  256.2 173.6 %reduce-scatter.8.cloned.1.call-start = ((), (), s32[]{:S(2)}) async-start(), calls=%async_computation.9 | async-start | bytes 98304 | tf_op jit(solution)/shard_map/reduce_scatter | solution.py:62
  662.1 146.2 %all-to-all-start.3 = ((bf16[40,104,1536]{2,1,0:T(8,128)(2,1)}), bf16[40,104,1536]{2,1,0:T(8,128)(2,1)}, u32[]{:S(2)}, u32[]{:S(2)}) async-start(bf16[40,104,1536]{2,1,0:T(8,128)(2,1)} %bitcast.164), calls=%async_computation.4 | async-start | bytes 25559040 | tf_op jit(solution)/shard_map/all_to_all | solution.py:74
  668.4 160.4 %reduce-scatter.4.cloned.1.call-start = ((), (), s32[]{:S(2)}) async-start(), calls=%async_computation.7 | async-start | bytes 1179648 | tf_op jit(solution)/shard_map/reduce_scatter | solution.py:57
  672.4 197.1 %reduce-scatter.6.cloned.1.call-start = ((), (), s32[]{:S(2)}) async-start(), calls=%async_computation.8 | async-start | bytes 1179648 | tf_op jit(solution)/shard_map/reduce_scatter | solution.py:77
  821.9 6.0 copy-start.3
  827.6 61.3 %all-reduce.2.cloned.1.call-start = ((), (), s32[]{:S(2)}) async-start(), calls=%async_computation.10 | async-start | bytes 491520 | tf_op jit(solution)/shard_map/psum | solution.py:81
  830.5 11.8 %copy-start.1 = (bf16[4,10,104,256]{3,2,0,1:T(8,128)(2,1)S(1)}, bf16[4,10,104,256]{3,2,0,1:T(8,128)(2,1)}, u32[]{:S(2)}) copy-start(bf16[4,10,104,256]{3,2,0,1:T(8,128)(2,1)} %get-tuple-element.14) | copy-start | bytes 6389764
  842.3 11.8 %copy-start.7 = (bf16[10,4,104,256]{3,2,1,0:T(8,128)(2,1)S(1)}, bf16[10,4,104,256]{3,2,1,0:T(8,128)(2,1)}, u32[]{:S(2)}) copy-start(bf16[10,4,104,256]{3,2,1,0:T(8,128)(2,1)} %fusion.39) | copy-start | bytes 6389764
  854.0 15.5 %copy-start.5 = (bf16[64,1536]{1,0:T(8,128)(2,1)S(1)}, bf16[64,1536]{1,0:T(8,128)(2,1)}, u32[]{:S(2)}) copy-start(bf16[64,1536]{1,0:T(8,128)(2,1)} %param.12) | copy-start | bytes 589828
Sparse Core Ops, SparseCore 0:
  414.7 7.7 reduce-scatter.7
  672.5 16.4 reduce-scatter.3
  827.7 15.0 reduce-scatter.5
  846.3 42.5 all-reduce.1
where the time goes:
time: 901 us; the launch traced here: 897 us
  blocking collectives  314 us (35%)
  waiting for transfers between devices  284 us (32%)
  matrix products  132 us (15%)
  local copies, waits for them, and re-layouts  106 us (12%)
  other arithmetic  33.9 us (4%)
  between operations  14.4 us (2%)
  starting transfers between devices  13.5 us (1%)
    all_to_all x1, blocking collectives, device_step(): lax.all_to_all(x_send.reshape(experts, cap_slots, d_model), 'ep', 0, 0, t...  144 us
    all_to_all x1, blocking collectives, device_step(): lax.all_to_all(do_send.reshape(experts, cap_slots, d_model), 'ep', 0, 0,...  144 us
    all_to_all x1, waiting for transfers between devices, device_step(): lax.all_to_all(dx_part.reshape(experts, cap_slots, d_model), 'ep', 0, 0,...  136 us
    all_to_all x1, waiting for transfers between devices, device_step(): lax.all_to_all(out_part.reshape(experts, cap_slots, d_model), 'ep', 0, 0,...  130 us
  transfers between devices with their start and end apart: 6, of which 3 were waited for; matrix products, arithmetic and copies ran while one was open for 9% of the time, Pallas kernels for 0%

commit v1 on v0

v1 whole, which is shorter than its diff:
```python
import functools

import jax
import jax.numpy as jnp
from jax import lax
from jax.experimental import pallas as pl
from jax.experimental.pallas import tpu as pltpu
from jax.sharding import PartitionSpec as P

MESH = pl.DeviceIdType.MESH
F32 = jnp.float32
BF16 = jnp.bfloat16
LANES = 128
GROUP = 16
OWN, DIAG, XN, YN = 0, 1, 2, 3


def dot(a, b):
    return jnp.dot(a, b, preferred_element_type=F32)


def dot_t(a, b):
    return lax.dot_general(a, b, (((1,), (1,)), ((), ())), preferred_element_type=F32)


def flip(index, bit):
    return index + bit - 2 * index * bit


def device_of(chip, other):
    ep, etp = lax.axis_index("ep"), lax.axis_index("etp")
    xb, yb = {OWN: (0, 0), DIAG: (1, 1), XN: (1, 0), YN: (0, 1)}[chip]
    return {"dp": lax.axis_index("dp"), "etp": flip(etp, yb), "ep": flip(ep // 2, xb) * 2 + flip(ep % 2, other)}


def rows_kernel(
    sizes, u_hbm, dy_hbm, ids_ref, wr_ref, wg_hbm, wu_hbm, wd_hbm,
    rows_out, ga_out, d1_out, d3_out, dl_out, own_out, send_out,
    ud, rt, w1, w3, w2, ga, d1, d3, ys, yo, yr, dgacc, dgb, dgr, dlb, wr16,
    in_sem, w_sem, ag_send, ag_recv, small_send, small_recv, pair_send, pair_recv, out_sem,
):
    tok, d_model, ffn, local_exp, experts, top_k = sizes
    half = tok // 2
    ep = lax.axis_index("ep")

    load_rows = [pltpu.make_async_copy(src, ud.at[k, pl.ds(0, tok), :], in_sem.at[k]) for k, src in enumerate((u_hbm, dy_hbm))]
    for c in load_rows:
        c.start()

    def load_w(e):
        cols = pl.ds(pl.multiple_of(e * ffn, ffn), ffn)
        return [
            pltpu.make_async_copy(wg_hbm.at[e], w1.at[:, cols], w_sem.at[0, e]),
            pltpu.make_async_copy(wu_hbm.at[e], w3.at[:, cols], w_sem.at[1, e]),
            pltpu.make_async_copy(wd_hbm.at[e], w2.at[cols, :], w_sem.at[2, e]),
        ]

    for e in range(local_exp):
        for c in load_w(e):
            c.start()

    barrier = pltpu.get_barrier_semaphore()
    others = [(chip, o) for chip in (OWN, DIAG, XN, YN) for o in (0, 1) if (chip, o) != (OWN, 0)]
    for chip, o in others:
        pl.semaphore_signal(barrier, inc=1, device_id=device_of(chip, o), device_id_type=MESH)

    lane40 = lax.broadcasted_iota(jnp.int32, (experts, LANES), 1) % 64
    row40 = lax.broadcasted_iota(jnp.int32, (experts, LANES), 0)
    spread = (row40 == (lane40 // GROUP) * local_exp + lane40 % GROUP) & (lane40 % GROUP < local_exp)
    wr16[...] = dot(wr_ref[...], jnp.where(spread, 1.0, 0.0).astype(BF16)).astype(BF16)
    for c in load_rows:
        c.wait()
    logits = dot(ud[0, 0:tok, :], wr16[...])
    lane = lax.broadcasted_iota(jnp.int32, (tok, LANES), 1)
    slot = lane % 64
    valid = slot % GROUP < local_exp
    logits = jnp.where(valid, logits, -1e30)
    top = jnp.max(logits, axis=1, keepdims=True)
    expo = jnp.where(valid, jnp.exp(logits - top), 0.0)
    prob = expo / jnp.sum(jnp.where(lane < 64, expo, 0.0), axis=1, keepdims=True)
    expert_of = jnp.where(valid, (slot // GROUP) * local_exp + slot % GROUP, -1)
    chosen = jnp.zeros((tok, LANES), jnp.bool_)
    ids = ids_ref[...]
    for j in range(top_k):
        chosen = chosen | (ids[:, j : j + 1] == expert_of)
    rt[0:tok, :] = jnp.where((lane < 64) | chosen, prob, -1.0)

    pl.semaphore_wait(barrier, len(others))

    def gather_copies(i, src, dst, count, dev):
        return [
            pltpu.make_async_remote_copy(rt.at[pl.ds(src, count), :], rt.at[pl.ds(dst, count), :], ag_send.at[0, i], ag_recv.at[0, i], device_id=dev, device_id_type=MESH),
            pltpu.make_async_remote_copy(ud.at[:, pl.ds(src, count), :], ud.at[:, pl.ds(dst, count), :], ag_send.at[1, i], ag_recv.at[1, i], device_id=dev, device_id_type=MESH),
        ]

    def xy_row(p, k):
        return 4 * tok + 2 * tok * p + half * k

    partner = device_of(OWN, 1)
    to_partner = gather_copies(0, 0, tok, tok, partner)
    to_x = [gather_copies(1 + p, half * p, xy_row(p, 0), half, device_of(XN, 0)) for p in (0, 1)]
    to_y = [gather_copies(3 + p, half * p, xy_row(p, 2), half, device_of(YN, 0)) for p in (0, 1)]
    to_d = gather_copies(5, 0, 2 * tok, tok, device_of(DIAG, 0))
    fwd_x = [gather_copies(6 + p, xy_row(p, 0), xy_row(p, 1), half, partner) for p in (0, 1)]
    fwd_y = [gather_copies(8 + p, xy_row(p, 2), xy_row(p, 3), half, partner) for p in (0, 1)]
    fwd_d = gather_copies(10, 2 * tok, 3 * tok, tok, partner)

    def start(copies):
        for c in copies:
            c.start()

    def wait_recv(copies):
        for c in copies:
            c.wait_recv()

    start(to_partner)
    for p in (0, 1):
        start(to_x[p])
        start(to_y[p])
    start(to_d)

    def expert_rows(row, e):
        rows = pl.ds(row, 2 * tok)
        cols = pl.ds(pl.multiple_of(e * ffn, ffn), ffn)
        h1 = dot(ud[0, rows, :], w1[:, cols]).astype(BF16).astype(F32)
        h3 = dot(ud[0, rows, :], w3[:, cols]).astype(BF16).astype(F32)
        da = dot_t(ud[1, rows, :], w2[cols, :])
        lanes = lax.broadcasted_iota(jnp.int32, (2 * tok, LANES), 1)
        mine = lanes == ep * GROUP + e
        gate = jnp.sum(jnp.where(lanes == 64 + ep * GROUP + e, rt[rows, :], 0.0), axis=1, keepdims=True)
        on = gate >= 0.0
        sig = jax.nn.sigmoid(h1)
        silu = h1 * sig
        act = (silu * h3).astype(BF16).astype(F32)
        ga[rows, cols] = jnp.where(on, gate * act, 0.0).astype(BF16)
        dgate = jnp.sum(act * da, axis=1, keepdims=True)
        dgacc[...] = jnp.where(mine, dgate, dgacc[...])
        da = (gate * da).astype(BF16).astype(F32)
        d1[rows, cols] = jnp.where(on, da * h3 * sig * (1.0 + h1 * (1.0 - sig)), 0.0).astype(BF16)
        d3[rows, cols] = jnp.where(on, da * silu, 0.0).astype(BF16)

    def rows_pass(row, first=False):
        dgacc[...] = jnp.zeros_like(dgacc)

        def body(i, carry):
            for k in range(2):
                if first:
                    for c in load_w(2 * i + k):
                        c.wait()
            for k in range(2):
                expert_rows(row, 2 * i + k)
            return carry

        lax.fori_loop(0, local_exp // 2, body, 0)

    outs = []

    def write_out(row):
        i = row // (2 * tok)
        rows = pl.ds(row, 2 * tok)
        copies = [pltpu.make_async_copy(s.at[rows, :], d.at[rows, :], out_sem.at[k, i]) for k, (s, d) in enumerate(((ga, ga_out), (d1, d1_out), (d3, d3_out)))]
        copies.append(pltpu.make_async_copy(ud.at[:, rows, :], rows_out.at[:, rows, :], out_sem.at[3, i]))
        start(copies)
        outs.extend(copies)

    def small(i, src, dst, dev):
        return pltpu.make_async_remote_copy(src, dst, small_send.at[i], small_recv.at[i], device_id=dev, device_id_type=MESH)

    dg_copies = {(chip, o): small(2 * chip + o, dgb.at[2 * chip + o], dgr.at[2 * chip + o], device_of(chip, o)) for chip, o in others}
    dl_copies = {(chip, o): small(8 + 2 * chip + o, dlb.at[0], dlb.at[2 * chip + o], device_of(chip, o)) for chip, o in others}

    to_partner[0].wait_recv()
    to_partner[1].wait_recv()
    rows_pass(0, first=True)
    write_out(0)
    dgb[0] = dgacc[0:tok, :]
    dgb[1] = dgacc[tok : 2 * tok, :]
    dg_copies[(OWN, 1)].start()

    for p in (0, 1):
        wait_recv(to_x[p])
        start(fwd_x[p])
        wait_recv(to_y[p])
        start(fwd_y[p])
        wait_recv(fwd_x[p])
        wait_recv(fwd_y[p])
        rows_pass(4 * tok + 2 * tok * p)
        write_out(4 * tok + 2 * tok * p)
        for k in range(4):
            dgb[4 + k, half * p : half * (p + 1), :] = dgacc[half * k : half * (k + 1), :]
    for chip in (XN, YN):
        for o in (0, 1):
            dg_copies[(chip, o)].start()

    def store_xy(k, tile, cols):
        for p in (0, 1):
            for c in (0, 1):
                at = 2 * tok * p + 2 * half * c
                ys[XN + c, k, half * p : half * (p + 1), cols] = tile[at : at + half]
                yo[XN + c, k, half * p : half * (p + 1), cols] = tile[at + half : at + 2 * half].astype(BF16)

    def store_own(k, tile, cols):
        for c in (0, 1):
            at = 2 * tok * c
            ys[OWN + c, k, :, cols] = tile[at : at + tok]
            yo[OWN + c, k, :, cols] = tile[at + tok : at + 2 * tok].astype(BF16)

    def sums_pass(row, store, lo, hi):
        rows = pl.ds(row, 4 * tok)
        width = 256

        def body(n, carry):
            cols = pl.ds(pl.multiple_of(n * width, width), width)
            store(0, dot(ga[rows, :], w2[:, cols]), cols)
            store(1, dot_t(d1[rows, :], w1[cols, :]) + dot_t(d3[rows, :], w3[cols, :]), cols)
            return carry

        lax.fori_loop(lo, hi, body, 0)

    pair = [
        pltpu.make_async_remote_copy(yo.at[pl.ds(2 * i, 2)], yr.at[pl.ds(2 * i, 2)], pair_send.at[i], pair_recv.at[i], device_id=partner, device_id_type=MESH)
        for i in (0, 1)
    ]
    steps = d_model // 256
    sums_pass(4 * tok, store_xy, 0, steps)
    pair[1].start()

    wait_recv(to_d)
    start(fwd_d)
    wait_recv(fwd_d)
    rows_pass(2 * tok)
    write_out(2 * tok)
    dgb[2] = dgacc[0:tok, :]
    dgb[3] = dgacc[tok : 2 * tok, :]
    for o in (0, 1):
        dg_copies[(DIAG, o)].start()
    sums_pass(0, store_own, 0, steps // 2)

    for c in dg_copies.values():
        c.wait_recv()
    dgate = dgb[0]
    for chip, o in others:
        dgate = dgate + dgr[2 * chip + o]
    own_rt = rt[0:tok, :]
    left = lane < 64
    prob = jnp.where(left, own_rt, 0.0)
    dprob = jnp.where(left & (pltpu.roll(own_rt, 64, 1) >= 0.0), dgate, 0.0)
    dlogit = prob * (dprob - jnp.sum(prob * dprob, axis=1, keepdims=True))
    high = dlogit.astype(BF16)
    low = dlogit - high.astype(F32)
    dlb[0] = jnp.where(left, high.astype(F32), pltpu.roll(low, 64, 1)).astype(BF16)
    for c in dl_copies.values():
        c.start()

    sums_pass(0, store_own, steps // 2, steps)
    pair[0].start()
    du_router = dot_t(dlb[0], wr16[...])

    pair[1].wait_recv()
    for k in (0, 1):
        send_out[1, k] = (ys[XN, k] + yr[XN, k].astype(F32)).astype(BF16)
        send_out[2, k] = (ys[YN, k] + yr[YN, k].astype(F32)).astype(BF16)
    for c in dl_copies.values():
        c.wait_recv()
    dl_out[0 : 2 * tok, :] = dlb[0:2].reshape(2 * tok, LANES)
    dl_out[2 * tok : 4 * tok, :] = dlb[2:4].reshape(2 * tok, LANES)
    for p in (0, 1):
        for k in range(4):
            at = 4 * tok + 2 * tok * p + half * k
            dl_out[at : at + half, :] = dlb[4 + k, half * p : half * (p + 1), :]
    pair[0].wait_recv()
    for k in (0, 1):
        send_out[0, k] = (ys[DIAG, k] + yr[DIAG, k].astype(F32)).astype(BF16)
    own_out[0] = ys[OWN, 0] + yr[OWN, 0].astype(F32) + ud[0, 0:tok, :].astype(F32)
    own_out[1] = ys[OWN, 1] + yr[OWN, 1].astype(F32) + ud[1, 0:tok, :].astype(F32) + du_router

    for copies in (to_partner, *to_x, *to_y, to_d, *fwd_x, *fwd_y, fwd_d):
        for c in copies:
            c.wait_send()
    for c in (*dg_copies.values(), *dl_copies.values(), *pair):
        c.wait_send()
    for c in outs:
        c.wait()


def grads_kernel(local_exp, rows_ref, ga_ref, d1_ref, d3_ref, dl_ref, dwg_ref, dwu_ref, dwd_ref, dwr_ref, xt):
    @pl.when(pl.program_id(0) == 0)
    def _():
        xt[...] = rows_ref[0].T
        wide = dot(xt[...], dl_ref[...])
        wide = wide + pltpu.roll(wide, 64, 1)
        lane = lax.broadcasted_iota(jnp.int32, wide.shape, 1)
        out = wide
        for g in range(1, dwr_ref.shape[1] // local_exp):
            out = jnp.where(lane >= g * local_exp, pltpu.roll(wide, LANES - g * (GROUP - local_exp), 1), out)
        dwr_ref[...] = out[:, : dwr_ref.shape[1]]

    dwg_ref[0] = dot(xt[...], d1_ref[...])
    dwu_ref[0] = dot(xt[...], d3_ref[...])
    dwd_ref[0] = lax.dot_general(ga_ref[...], rows_ref[1], (((0,), (0,)), ((), ())), preferred_element_type=F32)


def solution(mesh):
    tok_spec = P(("dp", "ep", "etp"), None)
    col_spec = P("ep", None, "etp")
    row_spec = P("ep", "etp", None)
    in_specs = (tok_spec, tok_spec, tok_spec, P(None, None), col_spec, col_spec, row_spec)
    out_specs = (tok_spec, tok_spec, P(("dp", "ep"), None, "etp"), P(("dp", "ep"), None, "etp"), P(("dp", "ep"), "etp", None), P("dp", None))

    def device_step(u_loc, dy_loc, ids_loc, w_router, w_gate, w_up, w_down):
        tok, d_model = u_loc.shape
        top_k = ids_loc.shape[1]
        experts = w_router.shape[1]
        local_exp, _, ffn = w_gate.shape
        rows = 8 * tok
        wide = local_exp * ffn
        any_spec = pl.BlockSpec(memory_space=pl.ANY)
        vmem_spec = pl.BlockSpec(memory_space=pltpu.VMEM)
        S = jax.ShapeDtypeStruct
        ud, ga, d1, d3, dl, own, send = pl.pallas_call(
            functools.partial(rows_kernel, (tok, d_model, ffn, local_exp, experts, top_k)),
            name="expert_rows",
            in_specs=[any_spec, any_spec, vmem_spec, vmem_spec, any_spec, any_spec, any_spec],
            out_specs=[any_spec] * 4 + [vmem_spec] * 3,
            out_shape=[
                S((2, rows, d_model), BF16), S((rows, wide), BF16), S((rows, wide), BF16), S((rows, wide), BF16),
                S((rows, LANES), BF16), S((2, tok, d_model), F32), S((3, 2, tok, d_model), BF16),
            ],
            scratch_shapes=[
                pltpu.VMEM((2, rows, d_model), BF16),
                pltpu.VMEM((rows, LANES), F32),
                pltpu.VMEM((d_model, wide), BF16), pltpu.VMEM((d_model, wide), BF16), pltpu.VMEM((wide, d_model), BF16),
                pltpu.VMEM((rows, wide), BF16), pltpu.VMEM((rows, wide), BF16), pltpu.VMEM((rows, wide), BF16),
                pltpu.VMEM((4, 2, tok, d_model), F32),
                pltpu.VMEM((4, 2, tok, d_model), BF16), pltpu.VMEM((4, 2, tok, d_model), BF16),
                pltpu.VMEM((2 * tok, LANES), F32),
                pltpu.VMEM((8, tok, LANES), F32), pltpu.VMEM((8, tok, LANES), F32),
                pltpu.VMEM((8, tok, LANES), BF16),
                pltpu.VMEM((d_model, LANES), BF16),
                pltpu.SemaphoreType.DMA((2,)), pltpu.SemaphoreType.DMA((3, local_exp)),
                pltpu.SemaphoreType.DMA((2, 11)), pltpu.SemaphoreType.DMA((2, 11)),
                pltpu.SemaphoreType.DMA((16,)), pltpu.SemaphoreType.DMA((16,)),
                pltpu.SemaphoreType.DMA((2,)), pltpu.SemaphoreType.DMA((2,)),
                pltpu.SemaphoreType.DMA((4, 4)),
            ],
            compiler_params=pltpu.CompilerParams(collective_id=0, has_side_effects=True, vmem_limit_bytes=62 * 1024 * 1024),
        )(u_loc, dy_loc, ids_loc, w_router, w_gate, w_up, w_down)

        n_ep, n_etp = lax.axis_size("ep"), lax.axis_size("etp")
        got_x = lax.ppermute(send[1], "ep", [(i, i ^ 2) for i in range(n_ep)])
        got_y = lax.ppermute(send[2], "etp", [(i, i ^ 1) for i in range(n_etp)])
        got_d = lax.ppermute(send[0], ("etp", "ep"), [(i, i ^ (n_ep + 2)) for i in range(n_ep * n_etp)])

        col_block = pl.BlockSpec((rows, ffn), lambda e: (0, e))
        dwg, dwu, dwd, dwr = pl.pallas_call(
            functools.partial(grads_kernel, local_exp),
            name="weight_grads",
            grid=(local_exp,),
            in_specs=[
                pl.BlockSpec((2, rows, d_model), lambda e: (0, 0, 0)),
                col_block, col_block, col_block,
                pl.BlockSpec((rows, LANES), lambda e: (0, 0)),
            ],
            out_specs=[
                pl.BlockSpec((1, d_model, ffn), lambda e: (e, 0, 0)),
                pl.BlockSpec((1, d_model, ffn), lambda e: (e, 0, 0)),
                pl.BlockSpec((1, ffn, d_model), lambda e: (e, 0, 0)),
                pl.BlockSpec((d_model, experts), lambda e: (0, 0)),
            ],
            out_shape=[S((local_exp, d_model, ffn), F32), S((local_exp, d_model, ffn), F32), S((local_exp, ffn, d_model), F32), S((d_model, experts), F32)],
            scratch_shapes=[pltpu.VMEM((d_model, rows), BF16)],
            compiler_params=pltpu.CompilerParams(vmem_limit_bytes=48 * 1024 * 1024),
            cost_estimate=pl.CostEstimate(flops=3 * 2 * rows * wide * d_model, bytes_accessed=12 * wide * d_model + 10 * rows * wide, transcendentals=0),
        )(ud, ga, d1, d3, dl)

        total = own + got_x.astype(F32) + got_y.astype(F32) + got_d.astype(F32)
        return total[0].astype(BF16), total[1].astype(BF16), dwg, dwu, dwd, dwr

    return jax.shard_map(device_step, mesh=mesh, in_specs=in_specs, out_specs=out_specs, check_vma=False)
```

time: 901 us -> 103 us (0.11)
  blocking collectives: 314 us -> 0 us
  waiting for transfers between devices: 284 us -> 0.01 us
  matrix products: 132 us -> 0 us
  local copies, waits for them, and re-layouts: 106 us -> 11.4 us
  Pallas kernels: 0 us -> 87.3 us
  other arithmetic: 33.9 us -> 0.17 us
  between operations: 14.4 us -> 0.67 us
  starting transfers between devices: 13.5 us -> 3.49 us
    all_to_all x2 -> x0, blocking collectives: 289 us -> none  [the longest x1 144 us: device_step(): lax.all_to_all(x_send.reshape(experts, cap_slots, d_model), 'ep', 0, 0, t...]
    all_to_all x2 -> x0, waiting for transfers between devices: 266 us -> none  [the longest x1 136 us: device_step(): lax.all_to_all(dx_part.reshape(experts, cap_slots, d_model), 'ep', 0, 0,...]
    dot_general x15 -> x0, matrix products: 132 us -> none  [the longest x1 17.6 us: device_step(): jnp.einsum('secf,edf->secd', d_up_h, w_up, preferred_element_type=jnp.flo...]
    pallas_call x0 -> x2, Pallas kernels: none -> 87.3 us  [the longest x1 66.6 us: device_step(): pl.pallas_call(functools.partial(rows_kernel, (tok, d_model, ffn, local_e...]
    gather x10 -> x0, local copies, waits for them, and re-layouts: 76.2 us -> none  [the longest x1 15 us: device_step(): jnp.take(gate_grp.reshape(-1), slot_pair, mode='fill', fill_value=0.0)]
    all_gather x4 -> x0, blocking collectives: 25.2 us -> none  [the longest x1 8.6 us: device_step(): dy_grp = lax.all_gather(dy_loc, 'etp', axis=0, tiled=True)]
    convert_element_type x2 -> x1, local copies, waits for them, and re-layouts: 21.6 us -> 0.77 us  [device_step(): return (total[0].astype(BF16), total[1].astype(BF16), dwg, dwu, dwd, dwr)]
    psum x1 -> x0, waiting for transfers between devices: 17.4 us -> none  [device_step(): lax.psum(jnp.einsum('td,te->de', u_loc, d_logit, preferred_element_type=j...]
  transfers between devices with their start and end apart: 6 -> 3, of which waited for: 3 -> 0; matrix products, arithmetic and copies ran while one was open for 9% -> 1% of each run, Pallas kernels for 0% -> 20%
where the time goes in v1:
time: 103 us
  Pallas kernels  87.3 us (85%)
  local copies, waits for them, and re-layouts  11.4 us (11%)
  starting transfers between devices  3.49 us (3%)
    pallas_call x1, Pallas kernels, device_step(): pl.pallas_call(functools.partial(rows_kernel, (tok, d_model, ffn, local_e...  66.6 us
    pallas_call x1, Pallas kernels, device_step(): pl.pallas_call(functools.partial(grads_kernel, local_exp), name='weight_g...  20.7 us
    unnamed x11, local copies, waits for them, and re-layouts  8.53 us
    squeeze x1, local copies, waits for them, and re-layouts, device_step(): got_x = lax.ppermute(send[1], 'ep', [(i, i ^ 2) for i in range(n_ep)])  2.11 us
  transfers between devices with their start and end apart: 3, of which 0 were waited for; matrix products, arithmetic and copies ran while one was open for 1% of the time, Pallas kernels for 20%

profile of v1, /device:TPU:0, one launch (start us, length us, event | category | flops | bytes accessed | tf_op | source)
XLA Modules:
  0.0 103.0 jit_solution(15747830775137703179)
XLA Ops:
  0.6 1.4 %copy.13.ids_ref = s32[64,8]{1,0:T(8,128)} copy(s32[64,8]{0,1:T(8,128)} %param.9) | data formatting | bytes 4096 | tf_op args[2]
  2.0 1.8 %copy.14.wr_ref = bf16[1536,40]{1,0:T(8,128)(2,1)} copy(bf16[1536,40]{0,1:T(8,128)(2,1)} %param.10) | data formatting | bytes 245760 | tf_op args[3]
  3.8 66.6 %expert_rows.1 = (bf16[2,512,1536]{2,1,0:T(8,128)(2,1)}, bf16[512,2560]{1,0:T(8,128)(2,1)}, bf16[512,2560]{1,0:T(8,128)(2,1)}, bf16[512,2560]{1,0:T(8,128)(2,1)}...) custom-call(bf16[64,1536]{1,0:T(8,128)(2,1)} %u_hbm.1, ...), custom_call_target="tpu_custom_call" | custom-call | tf_op jit(solution)/shard_map/expert_rows/pallas_call | solution.py:320
  70.4 2.1 %slice_bitcast_fusion.2 = (bf16[2,64,1536]{2,1,0:T(8,128)(2,1)}, bf16[2,64,1536]{2,1,0:T(8,128)(2,1)S(1)}, bf16[2,64,1536]{2,1,0:T(8,128)(2,1)S(1)}) fusion(bf16[3,2,64,1536]{3,2,1,0:T(8,128)(2,1)} %get-tuple-element.18), kind=kLoop, calls=%fused_computation.3 | loop fusion | bytes 2359296 | tf_op jit(solution)/shard_map/squeeze | solution.py:350
  72.5 1.3 %collective-permute-start = (bf16[2,64,1536]{2,1,0:T(8,128)(2,1)}, bf16[2,64,1536]{2,1,0:T(8,128)(2,1)S(1)}, u32[]{:S(2)}, u32[]{:S(2)}) collective-permute-start(bf16[2,64,1536]{2,1,0:T(8,128)(2,1)} %get-tuple-element.34), channel_id=1, source_target_pairs={{0,2},{1,3},{2,0},{3,1},{4,6},{5,7},{6,4},{7,5}} | collective-permute-start | bytes 1179656 | tf_op jit(solution)/shard_map/ppermute | solution.py:350
  73.8 1.5 %collective-permute-start.2 = (bf16[2,64,1536]{2,1,0:T(8,128)(2,1)S(1)}, bf16[2,64,1536]{2,1,0:T(8,128)(2,1)S(1)}, u32[]{:S(2)}, u32[]{:S(2)}) collective-permute-start(bf16[2,64,1536]{2,1,0:T(8,128)(2,1)S(1)} %get-tuple-element.35), channel_id=1, source_target_pairs={{0,6},{1,7},{2,4},{3,5},{4,2},{5,3},{6,0},{7,1}} | collective-permute-start | bytes 1179656 | tf_op jit(solution)/shard_map/ppermute | solution.py:352
  75.3 0.7 collective-permute-start.1
  76.0 0.0 copy-start
  76.0 1.7 %copy-done = bf16[512,2560]{1,0:T(8,128)(2,1)S(1)} copy-done((bf16[512,2560]{1,0:T(8,128)(2,1)S(1)}, bf16[512,2560]{1,0:T(8,128)(2,1)}, u32[]{:S(2)}) %copy-start) | copy-done | bytes 2621464
  77.8 0.0 copy-start.1
  77.8 1.7 %copy-done.1 = bf16[512,2560]{1,0:T(8,128)(2,1)S(1)} copy-done((bf16[512,2560]{1,0:T(8,128)(2,1)S(1)}, bf16[512,2560]{1,0:T(8,128)(2,1)}, u32[]{:S(2)}) %copy-start.1) | copy-done | bytes 2621464
  79.5 0.0 copy-start.2
  79.5 0.9 copy-done.2
  80.4 0.0 copy-start.3
  80.4 20.7 %weight_grads.1 = (f32[10,1536,256]{2,1,0:T(8,128)}, f32[10,1536,256]{2,1,0:T(8,128)}, f32[10,256,1536]{2,1,0:T(8,128)}, f32[1536,40]{1,0:T(8,128)S(1)}) custom-call(bf16[2,512,1536]{2,1,0:T(8,128)(2,1)} %get-tuple-element.19.rows_ref, bf16[512,2560]{1,0:T(8,128)(2,1)S(1)} %copy-done, bf16[512,2560]{1,0:T(8,128)(2,1)S(1)} %copy-done.1, ...), custom_call_target="tpu_custom_call" | custom-call | flops 12079595520 | bytes 60293120 | tf_op jit(solution)/shard_map/weight_grads/pallas_call | solution.py:355
  101.1 0.9 copy.15
  102.1 0.0 collective-permute-done
  102.1 0.0 collective-permute-done.2
  102.1 0.0 collective-permute-done.1
  102.1 0.0 copy-done.3
  102.1 0.2 add_convert_fusion
  102.3 0.8 slice_bitcast_fusion.3
Async XLA Ops:
  72.5 29.5 %collective-permute-start = (bf16[2,64,1536]{2,1,0:T(8,128)(2,1)}, bf16[2,64,1536]{2,1,0:T(8,128)(2,1)S(1)}, u32[]{:S(2)}, u32[]{:S(2)}) collective-permute-start(bf16[2,64,1536]{2,1,0:T(8,128)(2,1)} %get-tuple-element.34), channel_id=1, source_target_pairs={{0,2},{1,3},{2,0},{3,1},{4,6},{5,7},{6,4},{7,5}} | collective-permute-start | bytes 1179656 | tf_op jit(solution)/shard_map/ppermute | solution.py:350
  73.8 28.3 %collective-permute-start.2 = (bf16[2,64,1536]{2,1,0:T(8,128)(2,1)S(1)}, bf16[2,64,1536]{2,1,0:T(8,128)(2,1)S(1)}, u32[]{:S(2)}, u32[]{:S(2)}) collective-permute-start(bf16[2,64,1536]{2,1,0:T(8,128)(2,1)S(1)} %get-tuple-element.35), channel_id=1, source_target_pairs={{0,6},{1,7},{2,4},{3,5},{4,2},{5,3},{6,0},{7,1}} | collective-permute-start | bytes 1179656 | tf_op jit(solution)/shard_map/ppermute | solution.py:352
  75.3 26.8 %collective-permute-start.1 = (bf16[2,64,1536]{2,1,0:T(8,128)(2,1)S(1)}, bf16[2,64,1536]{2,1,0:T(8,128)(2,1)S(1)}, u32[]{:S(2)}, u32[]{:S(2)}) collective-permute-start(bf16[2,64,1536]{2,1,0:T(8,128)(2,1)S(1)} %get-tuple-element.36), channel_id=1, source_target_pairs={{0,4},{4,0},{1,5},{5,1},{2,6},{6,2},{3,7},{7,3}} | collective-permute-start | bytes 1179656 | tf_op jit(solution)/shard_map/ppermute | solution.py:351
  76.0 1.7 %copy-start = (bf16[512,2560]{1,0:T(8,128)(2,1)S(1)}, bf16[512,2560]{1,0:T(8,128)(2,1)}, u32[]{:S(2)}) copy-start(bf16[512,2560]{1,0:T(8,128)(2,1)} %get-tuple-element.20.ga_ref) | copy-start | bytes 7864324
  77.8 1.7 %copy-start.1 = (bf16[512,2560]{1,0:T(8,128)(2,1)S(1)}, bf16[512,2560]{1,0:T(8,128)(2,1)}, u32[]{:S(2)}) copy-start(bf16[512,2560]{1,0:T(8,128)(2,1)} %get-tuple-element.21.d1_ref) | copy-start | bytes 7864324
  79.5 0.9 copy-start.2
  80.4 21.7 %copy-start.3 = (f32[2,64,1536]{2,1,0:T(8,128)S(1)}, f32[2,64,1536]{2,1,0:T(8,128)}, u32[]{:S(2)}) copy-start(f32[2,64,1536]{2,1,0:T(8,128)} %get-tuple-element.17) | copy-start | bytes 2359300

commit v2 on v1

v2 whole, which is shorter than its diff:
```python
import functools

import jax
import jax.numpy as jnp
from jax import lax
from jax.experimental import pallas as pl
from jax.experimental.pallas import tpu as pltpu
from jax.sharding import PartitionSpec as P

MESH = pl.DeviceIdType.MESH
F32 = jnp.float32
BF16 = jnp.bfloat16
LANES = 128
GROUP = 16
OWN, DIAG, XN, YN = 0, 1, 2, 3


def dot(a, b):
    return jnp.dot(a, b, preferred_element_type=F32)


def dot_t(a, b):
    return lax.dot_general(a, b, (((1,), (1,)), ((), ())), preferred_element_type=F32)


def flip(index, bit):
    return index + bit - 2 * index * bit


def device_of(chip, other):
    ep, etp = lax.axis_index("ep"), lax.axis_index("etp")
    xb, yb = {OWN: (0, 0), DIAG: (1, 1), XN: (1, 0), YN: (0, 1)}[chip]
    return {"dp": lax.axis_index("dp"), "etp": flip(etp, yb), "ep": flip(ep // 2, xb) * 2 + flip(ep % 2, other)}


def rows_kernel(
    sizes, u_hbm, dy_hbm, ids_ref, wr_ref, wg_hbm, wu_hbm, wd_hbm,
    u_out, dy_out, ga_out, d1_out, d3_out, dl_out, own_out, send_out,
    u, dy, rt, w1, w3, w2, ga, d1, d3, sg, ys, yo, yr, xs, xr, dgacc, dgb, dgr, dlb, wr16,
    in_sem, w_sem, ag_send, ag_recv, small_send, small_recv, pair_send, pair_recv, xy_send, xy_recv, out_sem,
):
    tok, d_model, ffn, local_exp, experts, top_k = sizes
    ep = lax.axis_index("ep")

    load_rows = [pltpu.make_async_copy(src, dst.at[pl.ds(0, tok), :], in_sem.at[k]) for k, (src, dst) in enumerate(((u_hbm, u), (dy_hbm, dy)))]
    for c in load_rows:
        c.start()

    def load_w(e):
        cols = pl.ds(pl.multiple_of(e * ffn, ffn), ffn)
        return [
            pltpu.make_async_copy(wg_hbm.at[e], w1.at[:, cols], w_sem.at[0, e]),
            pltpu.make_async_copy(wu_hbm.at[e], w3.at[:, cols], w_sem.at[1, e]),
            pltpu.make_async_copy(wd_hbm.at[e], w2.at[cols, :], w_sem.at[2, e]),
        ]

    barrier = pltpu.get_barrier_semaphore()
    others = [(chip, o) for chip in (OWN, DIAG, XN, YN) for o in (0, 1) if (chip, o) != (OWN, 0)]
    for chip, o in others:
        pl.semaphore_signal(barrier, inc=1, device_id=device_of(chip, o), device_id_type=MESH)

    slot40 = lax.broadcasted_iota(jnp.int32, (LANES, experts), 0) % 64
    col40 = lax.broadcasted_iota(jnp.int32, (LANES, experts), 1)
    spread = (col40 == (slot40 // GROUP) * local_exp + slot40 % GROUP) & (slot40 % GROUP < local_exp)
    wr16[...] = dot(jnp.where(spread, 1.0, 0.0).astype(BF16), wr_ref[...]).astype(BF16)
    slot_t = lax.broadcasted_iota(jnp.int32, (LANES, tok), 0) % 64
    expert_t = jnp.where(slot_t % GROUP < local_exp, (slot_t // GROUP) * local_exp + slot_t % GROUP, -1)
    chosen_t = jnp.zeros((LANES, tok), F32)
    for j in range(top_k):
        chosen_t = jnp.where(expert_t == ids_ref[j : j + 1, :], 1.0, chosen_t)
    chosen = chosen_t.T > 0.5
    lane = lax.broadcasted_iota(jnp.int32, (tok, LANES), 1)
    valid = lane % GROUP < local_exp
    for c in load_rows:
        c.wait()
    for which in (slice(0, 2), slice(2, 3)):
        for e in range(local_exp):
            for c in load_w(e)[which]:
                c.start()

    logits = jnp.where(valid, dot_t(u[0:tok, :], wr16[...]), -1e30)
    top = jnp.max(logits, axis=1, keepdims=True)
    expo = jnp.where(valid, jnp.exp(logits - top), 0.0)
    prob = expo / jnp.sum(jnp.where(lane < 64, expo, 0.0), axis=1, keepdims=True)
    rt[0:tok, :] = jnp.where((lane < 64) | chosen, prob, -1.0)

    pl.semaphore_wait(barrier, len(others))

    def block(chip, o):
        return pl.ds((2 * chip + o) * tok, tok)

    def gather(i, src, dst, dev):
        return [
            pltpu.make_async_remote_copy(ref.at[src, :], ref.at[dst, :], ag_send.at[k, i], ag_recv.at[k, i], device_id=dev, device_id_type=MESH)
            for k, ref in enumerate((rt, u, dy))
        ]

    partner = device_of(OWN, 1)
    to_partner = gather(0, block(OWN, 0), block(OWN, 1), partner)
    to_chip = {chip: gather(chip, block(OWN, 0), block(chip, 0), device_of(chip, 0)) for chip in (DIAG, XN, YN)}
    forward = {chip: gather(3 + chip, block(chip, 0), block(chip, 1), partner) for chip in (DIAG, XN, YN)}

    def start(copies):
        for c in copies:
            c.start()

    def wait_recv(copies):
        for c in copies:
            c.wait_recv()

    def send_part(k):
        for copies in (to_partner, to_chip[XN], to_chip[YN]):
            copies[k].start()

    send_part(0)
    send_part(1)

    def pass_on(chip, parts):
        for k in parts:
            to_chip[chip][k].wait_recv()
            forward[chip][k].start()

    def cols_of(e):
        return pl.ds(pl.multiple_of(e * ffn, ffn), ffn)

    def gate_of(rows, count, e):
        lanes = lax.broadcasted_iota(jnp.int32, (count, LANES), 1)
        return jnp.sum(jnp.where(lanes == 64 + ep * GROUP + e, rt[rows, :], 0.0), axis=1, keepdims=True)

    unroll = 5

    def over_experts(lo, hi, one, which=None):
        def body(i, carry):
            if which is not None:
                for k in range(unroll):
                    for c in load_w(i * unroll + k)[which]:
                        c.wait()
            for k in range(unroll):
                one(i * unroll + k)
            return carry

        lax.fori_loop(lo // unroll, hi // unroll, body, 0)

    def u_pass(row, count, lo, hi, first=False):
        rows = pl.ds(row, count)

        def one(e):
            cols = cols_of(e)
            h1 = dot(u[rows, :], w1[:, cols]).astype(BF16)
            h3 = dot(u[rows, :], w3[:, cols]).astype(BF16)
            d1[rows, cols] = h1
            d3[rows, cols] = h3
            gate = gate_of(rows, count, e)
            h1 = h1.astype(F32)
            sig = jax.nn.sigmoid(h1)
            sg[rows, cols] = sig
            act = (h1 * sig * h3.astype(F32)).astype(BF16).astype(F32)
            ga[rows, cols] = jnp.where(gate >= 0.0, gate * act, 0.0).astype(BF16)

        over_experts(lo, hi, one, slice(0, 2) if first else None)

    def dy_pass(row, count, first=False):
        rows = pl.ds(row, count)

        def one(e):
            cols = cols_of(e)
            da = dot_t(dy[rows, :], w2[cols, :])
            lanes = lax.broadcasted_iota(jnp.int32, (count, LANES), 1)
            gate = gate_of(rows, count, e)
            on = gate >= 0.0
            h1 = d1[rows, cols].astype(F32)
            h3 = d3[rows, cols].astype(F32)
            sig = sg[rows, cols]
            silu = h1 * sig
            act = (silu * h3).astype(BF16).astype(F32)
            dgate = jnp.sum(act * da, axis=1, keepdims=True)
            dgacc[...] = jnp.where(lanes == ep * GROUP + e, dgate, dgacc[...])
            da = (gate * da).astype(BF16).astype(F32)
            d1[rows, cols] = jnp.where(on, da * (h3 * (sig * (1.0 + h1 * (1.0 - sig)))), 0.0).astype(BF16)
            d3[rows, cols] = jnp.where(on, da * silu, 0.0).astype(BF16)

        dgacc[...] = jnp.zeros_like(dgacc)
        over_experts(0, local_exp, one, slice(2, 3) if first else None)

    outs = []

    def write_out(row, count, pairs, sem):
        rows = pl.ds(row, count)
        copies = [pltpu.make_async_copy(s.at[rows, :], d.at[rows, :], out_sem.at[sem, k]) for k, (s, d) in enumerate(pairs)]
        start(copies)
        outs.extend(copies)

    grads = ((ga, ga_out), (d1, d1_out), (d3, d3_out), (u, u_out), (dy, dy_out))

    def small(i, src, dst, dev):
        return pltpu.make_async_remote_copy(src, dst, small_send.at[i], small_recv.at[i], device_id=dev, device_id_type=MESH)

    dg_copies = {(chip, o): small(2 * chip + o, dgb.at[2 * chip + o], dgr.at[2 * chip + o], device_of(chip, o)) for chip, o in others}
    dl_copies = {(chip, o): small(8 + 2 * chip + o, dlb.at[0], dlb.at[2 * chip + o], device_of(chip, o)) for chip, o in others}

    def send_gates(chips):
        for i, chip in enumerate(chips):
            for o in (0, 1):
                k = 2 * i + o
                dgb[2 * chip + o] = dgacc[k * tok : (k + 1) * tok, :]
                if (chip, o) != (OWN, 0):
                    dg_copies[(chip, o)].start()

    def sums_pass(row, chips, lo, hi):
        rows = pl.ds(row, 4 * tok)
        width = 256
        for n in range(lo, hi):
            cols = pl.ds(n * width, width)
            y = dot(ga[rows, :], w2[:, cols])
            dx = dot_t(d1[rows, :], w1[cols, :]) + dot_t(d3[rows, :], w3[cols, :])
            for k, tile in enumerate((y, dx)):
                for i, chip in enumerate(chips):
                    at = 2 * tok * i
                    ys[chip, k, :, cols] = tile[at : at + tok]
                    yo[chip, k, :, cols] = tile[at + tok : at + 2 * tok].astype(BF16)

    pair = [
        pltpu.make_async_remote_copy(yo.at[pl.ds(2 * i, 2)], yr.at[pl.ds(2 * i, 2)], pair_send.at[i], pair_recv.at[i], device_id=partner, device_id_type=MESH)
        for i in (0, 1)
    ]
    xy = [
        pltpu.make_async_remote_copy(xs.at[i], xr.at[i], xy_send.at[i], xy_recv.at[i], device_id=device_of(chip, 0), device_id_type=MESH)
        for i, chip in enumerate((XN, YN))
    ]
    steps = d_model // 256

    wait_recv(to_partner[:2])
    u_pass(0, 2 * tok, 0, local_exp, first=True)
    send_part(2)

    for chip in (XN, YN):
        pass_on(chip, (0, 1))
    for chip in (XN, YN):
        wait_recv(forward[chip][:2])
    u_pass(4 * tok, 4 * tok, 0, unroll)
    start(to_chip[DIAG])
    for chip in (XN, YN):
        pass_on(chip, (2,))
    u_pass(4 * tok, 4 * tok, unroll, local_exp)
    for chip in (XN, YN):
        forward[chip][2].wait_recv()
    dy_pass(4 * tok, 4 * tok, first=True)
    write_out(4 * tok, 4 * tok, grads, 0)
    send_gates((XN, YN))
    sums_pass(4 * tok, (XN, YN), 0, steps - 2)
    pass_on(DIAG, (0, 1, 2))
    sums_pass(4 * tok, (XN, YN), steps - 2, steps)
    pair[1].start()

    wait_recv(forward[DIAG])
    to_partner[2].wait_recv()
    u_pass(2 * tok, 2 * tok, 0, local_exp)
    pair[1].wait_recv()
    for i, chip in enumerate((XN, YN)):
        for k in (0, 1):
            xs[i, k] = (ys[chip, k] + yr[chip, k].astype(F32)).astype(BF16)
        xy[i].start()
    dy_pass(0, 4 * tok)
    write_out(0, 4 * tok, grads, 1)
    send_gates((OWN, DIAG))
    sums_pass(0, (OWN, DIAG), 0, steps - 2)

    for c in dg_copies.values():
        c.wait_recv()
    dgate = dgb[0]
    for chip, o in others:
        dgate = dgate + dgr[2 * chip + o]
    own_rt = rt[0:tok, :]
    left = lane < 64
    prob = jnp.where(left, own_rt, 0.0)
    dprob = jnp.where(left & (pltpu.roll(own_rt, 64, 1) >= 0.0), dgate, 0.0)
    dlogit = prob * (dprob - jnp.sum(prob * dprob, axis=1, keepdims=True))
    high = dlogit.astype(BF16)
    low = dlogit - high.astype(F32)
    dlb[0] = jnp.where(left, high.astype(F32), pltpu.roll(low, 64, 1)).astype(BF16)
    start(dl_copies.values())

    sums_pass(0, (OWN, DIAG), steps - 2, steps)
    pair[0].start()
    du_router = dot(dlb[0], wr16[...])
    wait_recv(dl_copies.values())
    dl_out[...] = dlb[...].reshape(8 * tok, LANES)
    pair[0].wait_recv()
    for k in (0, 1):
        send_out[k] = (ys[DIAG, k] + yr[DIAG, k].astype(F32)).astype(BF16)
    wait_recv(xy)
    for k, base in enumerate((u[0:tok, :].astype(F32), dy[0:tok, :].astype(F32) + du_router)):
        own_out[k] = ys[OWN, k] + yr[OWN, k].astype(F32) + base + xr[0, k].astype(F32) + xr[1, k].astype(F32)

    for copies in (to_partner, *to_chip.values(), *forward.values(), dg_copies.values(), dl_copies.values(), pair, xy):
        for c in copies:
            c.wait_send()
    for c in outs:
        c.wait()


def grads_kernel(local_exp, u_ref, dy_ref, ga_ref, d1_ref, d3_ref, dl_ref, dwg_ref, dwu_ref, dwd_ref, dwr_ref, xt):
    def over_tokens(a, b):
        return lax.dot_general(a, b, (((0,), (0,)), ((), ())), preferred_element_type=F32)

    @pl.when(pl.program_id(0) == 0)
    def _():
        xt[...] = u_ref[...].T
        wide = over_tokens(dl_ref[...], u_ref[...])
        wide = wide[0:64] + wide[64:128]
        for g in range(dwr_ref.shape[0] // local_exp):
            dwr_ref[g * local_exp : (g + 1) * local_exp, :] = wide[g * GROUP : g * GROUP + local_exp]

    dwg_ref[0] = dot(xt[...], d1_ref[...])
    dwu_ref[0] = dot(xt[...], d3_ref[...])
    dwd_ref[0] = over_tokens(ga_ref[...], dy_ref[...])


def solution(mesh):
    tok_spec = P(("dp", "ep", "etp"), None)
    col_spec = P("ep", None, "etp")
    row_spec = P("ep", "etp", None)
    in_specs = (tok_spec, tok_spec, tok_spec, P(None, None), col_spec, col_spec, row_spec)
    out_specs = (tok_spec, tok_spec, P(("dp", "ep"), None, "etp"), P(("dp", "ep"), None, "etp"), P(("dp", "ep"), "etp", None), P("dp", None))

    def device_step(u_loc, dy_loc, ids_loc, w_router, w_gate, w_up, w_down):
        tok, d_model = u_loc.shape
        top_k = ids_loc.shape[1]
        experts = w_router.shape[1]
        local_exp, _, ffn = w_gate.shape
        rows = 8 * tok
        wide = local_exp * ffn
        any_spec = pl.BlockSpec(memory_space=pl.ANY)
        vmem_spec = pl.BlockSpec(memory_space=pltpu.VMEM)
        S = jax.ShapeDtypeStruct
        dma = pltpu.SemaphoreType.DMA
        u, dy, ga, d1, d3, dl, own, send = pl.pallas_call(
            functools.partial(rows_kernel, (tok, d_model, ffn, local_exp, experts, top_k)),
            name="expert_rows",
            in_specs=[any_spec, any_spec, vmem_spec, vmem_spec, any_spec, any_spec, any_spec],
            out_specs=[any_spec] * 5 + [vmem_spec] * 3,
            out_shape=[
                S((rows, d_model), BF16), S((rows, d_model), BF16),
                S((rows, wide), BF16), S((rows, wide), BF16), S((rows, wide), BF16),
                S((rows, LANES), BF16), S((2, tok, d_model), F32), S((2, tok, d_model), BF16),
            ],
            scratch_shapes=[
                pltpu.VMEM((rows, d_model), BF16), pltpu.VMEM((rows, d_model), BF16),
                pltpu.VMEM((rows, LANES), F32),
                pltpu.VMEM((d_model, wide), BF16), pltpu.VMEM((d_model, wide), BF16), pltpu.VMEM((wide, d_model), BF16),
                pltpu.VMEM((rows, wide), BF16), pltpu.VMEM((rows, wide), BF16), pltpu.VMEM((rows, wide), BF16), pltpu.VMEM((rows, wide), F32),
                pltpu.VMEM((4, 2, tok, d_model), F32),
                pltpu.VMEM((4, 2, tok, d_model), BF16), pltpu.VMEM((4, 2, tok, d_model), BF16),
                pltpu.VMEM((2, 2, tok, d_model), BF16), pltpu.VMEM((2, 2, tok, d_model), BF16),
                pltpu.VMEM((4 * tok, LANES), F32),
                pltpu.VMEM((8, tok, LANES), F32), pltpu.VMEM((8, tok, LANES), F32),
                pltpu.VMEM((8, tok, LANES), BF16),
                pltpu.VMEM((LANES, d_model), BF16),
                dma((2,)), dma((3, local_exp)), dma((3, 7)), dma((3, 7)), dma((16,)), dma((16,)),
                dma((2,)), dma((2,)), dma((2,)), dma((2,)), dma((2, 5)),
            ],
            compiler_params=pltpu.CompilerParams(collective_id=0, has_side_effects=True, vmem_limit_bytes=62 * 1024 * 1024),
        )(u_loc, dy_loc, ids_loc.T, w_router.T, w_gate, w_up, w_down)

        n_ep, n_etp = lax.axis_size("ep"), lax.axis_size("etp")
        got = lax.ppermute(send, ("etp", "ep"), [(i, i ^ (n_ep + 2)) for i in range(n_ep * n_etp)])

        col_block = pl.BlockSpec((rows, ffn), lambda e: (0, e))
        whole_rows = pl.BlockSpec((rows, d_model), lambda e: (0, 0))
        dwg, dwu, dwd, dwr = pl.pallas_call(
            functools.partial(grads_kernel, local_exp),
            name="weight_grads",
            grid=(local_exp,),
            in_specs=[whole_rows, whole_rows, col_block, col_block, col_block, pl.BlockSpec((rows, LANES), lambda e: (0, 0))],
            out_specs=[
                pl.BlockSpec((1, d_model, ffn), lambda e: (e, 0, 0)),
                pl.BlockSpec((1, d_model, ffn), lambda e: (e, 0, 0)),
                pl.BlockSpec((1, ffn, d_model), lambda e: (e, 0, 0)),
                pl.BlockSpec((experts, d_model), lambda e: (0, 0)),
            ],
            out_shape=[S((local_exp, d_model, ffn), F32), S((local_exp, d_model, ffn), F32), S((local_exp, ffn, d_model), F32), S((experts, d_model), F32)],
            scratch_shapes=[pltpu.VMEM((d_model, rows), BF16)],
            compiler_params=pltpu.CompilerParams(vmem_limit_bytes=62 * 1024 * 1024),
            cost_estimate=pl.CostEstimate(flops=3 * 2 * rows * wide * d_model, bytes_accessed=12 * wide * d_model + 10 * rows * wide, transcendentals=0),
        )(u, dy, ga, d1, d3, dl)

        y_loc = (own[0] + got[0].astype(F32)).astype(BF16)
        du_loc = (own[1] + got[1].astype(F32)).astype(BF16)
        return y_loc, du_loc, dwg, dwu, dwd, dwr.T

    return jax.shard_map(device_step, mesh=mesh, in_specs=in_specs, out_specs=out_specs, check_vma=False)
```

time: 103 us -> 75.3 us (0.73)
  Pallas kernels: 87.3 us -> 71.5 us
  local copies, waits for them, and re-layouts: 11.4 us -> 0.01 us
  starting transfers between devices: 3.49 us -> 1.91 us
    pallas_call x1, Pallas kernels: 66.6 us -> 50.6 us  [device_step(): pl.pallas_call(functools.partial(rows_kernel, (tok, d_model, ffn, local_e...]
    unnamed x11 -> x2, local copies, waits for them, and re-layouts: 8.53 us -> 0.01 us
    squeeze x1 -> x0, local copies, waits for them, and re-layouts: 2.11 us -> none  [device_step(): got_x = lax.ppermute(send[1], 'ep', [(i, i ^ 2) for i in range(n_ep)])]
    ppermute x3 -> x1, starting transfers between devices: 3.49 us -> 1.91 us  [device_step(): lax.ppermute(send, ('etp', 'ep'), [(i, i ^ n_ep + 2) for i in range(n_ep...]
  transfers between devices with their start and end apart: 3 -> 1, of which waited for: 0 -> 0; matrix products, arithmetic and copies ran while one was open for 1% -> 0% of each run, Pallas kernels for 20% -> 28%
where the time goes in v2:
time: 75.3 us; the launch traced here: 74.8 us
  Pallas kernels  71.5 us (95%)
  starting transfers between devices  1.91 us (3%)
  other arithmetic  0.81 us (1%)
    pallas_call x1, Pallas kernels, device_step(): pl.pallas_call(functools.partial(rows_kernel, (tok, d_model, ffn, local_e...  50.6 us
    pallas_call x1, Pallas kernels, device_step(): pl.pallas_call(functools.partial(grads_kernel, local_exp), name='weight_g...  20.9 us
    ppermute x1, starting transfers between devices, device_step(): lax.ppermute(send, ('etp', 'ep'), [(i, i ^ n_ep + 2) for i in range(n_ep...  1.91 us
  transfers between devices with their start and end apart: 1, of which 0 were waited for; matrix products, arithmetic and copies ran while one was open for 0% of the time, Pallas kernels for 28%

profile of v2, /device:TPU:0, one launch (start us, length us, event | category | flops | bytes accessed | tf_op | source)
XLA Modules:
  0.0 74.8 jit_solution(17449261129450056359)
XLA Ops:
  0.6 50.6 %expert_rows.1 = (bf16[512,1536]{1,0:T(8,128)(2,1)}, bf16[512,1536]{1,0:T(8,128)(2,1)}, bf16[512,2560]{1,0:T(8,128)(2,1)}, bf16[512,2560]{1,0:T(8,128)(2,1)}, bf...) custom-call(bf16[64,1536]{1,0:T(8,128)(2,1)} %u_hbm.1, ...), custom_call_target="tpu_custom_call" | custom-call | tf_op jit(solution)/shard_map/expert_rows/pallas_call | solution.py:337
  51.3 1.9 %collective-permute-start = (bf16[2,64,1536]{2,1,0:T(8,128)(2,1)}, bf16[2,64,1536]{2,1,0:T(8,128)(2,1)S(1)}, u32[]{:S(2)}, u32[]{:S(2)}) collective-permute-start(bf16[2,64,1536]{2,1,0:T(8,128)(2,1)} %get-tuple-element.19), channel_id=1, source_target_pairs={{0,6},{1,7},{2,4},{3,5},{4,2},{5,3},{6,0},{7,1}} | collective-permute-start | bytes 1179656 | tf_op jit(solution)/shard_map/ppermute | solution.py:366
  53.2 0.0 copy-start
  53.2 20.9 %weight_grads.1 = (f32[10,1536,256]{2,1,0:T(8,128)}, f32[10,1536,256]{2,1,0:T(8,128)}, f32[10,256,1536]{2,1,0:T(8,128)}, f32[40,1536]{1,0:T(8,128)}) custom-call(bf16[512,1536]{1,0:T(8,128)(2,1)} %get-tuple-element.20.u_ref, bf16[512,1536]{1,0:T(8,128)(2,1)} %get-tuple-element.21.dy_ref, bf16[512,2560]{1,0:T(8,128)(2,1)} %get-tuple-element.22.ga_ref, ...), custom_call_target="tpu_custom_call" | custom-call | flops 12079595520 | bytes 60293120 | tf_op jit(solution)/shard_map/weight_grads/pallas_call | solution.py:370
  74.0 0.0 collective-permute-done
  74.0 0.0 copy-done
  74.0 0.8 %fusion.1 = (bf16[64,1536]{1,0:T(8,128)(2,1)}, bf16[64,1536]{1,0:T(8,128)(2,1)}) fusion(f32[2,64,1536]{2,1,0:T(8,128)S(1)} %copy-done, bf16[2,64,1536]{2,1,0:T(8,128)(2,1)S(1)} %collective-permute-done), kind=kLoop, calls=%fused_computation.3 | loop fusion | flops 589824 | bytes 1572864 | tf_op jit(solution)/shard_map/convert_element_type | solution.py:388
Async XLA Ops:
  51.3 22.8 %collective-permute-start = (bf16[2,64,1536]{2,1,0:T(8,128)(2,1)}, bf16[2,64,1536]{2,1,0:T(8,128)(2,1)S(1)}, u32[]{:S(2)}, u32[]{:S(2)}) collective-permute-start(bf16[2,64,1536]{2,1,0:T(8,128)(2,1)} %get-tuple-element.19), channel_id=1, source_target_pairs={{0,6},{1,7},{2,4},{3,5},{4,2},{5,3},{6,0},{7,1}} | collective-permute-start | bytes 1179656 | tf_op jit(solution)/shard_map/ppermute | solution.py:366
  53.2 20.9 %copy-start = (f32[2,64,1536]{2,1,0:T(8,128)S(1)}, f32[2,64,1536]{2,1,0:T(8,128)}, u32[]{:S(2)}) copy-start(f32[2,64,1536]{2,1,0:T(8,128)} %get-tuple-element.18) | copy-start | bytes 2359300

commit v3 on v2

--- a/solution.py
+++ b/solution.py
@@ -73,10 +73,14 @@
     valid = lane % GROUP < local_exp
     for c in load_rows:
         c.wait()
-    for which in (slice(0, 2), slice(2, 3)):
-        for e in range(local_exp):
+    unroll = 5
+
+    def start_w(lo, hi, which):
+        for e in range(lo, hi):
             for c in load_w(e)[which]:
                 c.start()
+
+    start_w(0, unroll, slice(0, 2))
 
     logits = jnp.where(valid, dot_t(u[0:tok, :], wr16[...]), -1e30)
     top = jnp.max(logits, axis=1, keepdims=True)
@@ -85,6 +89,7 @@
     rt[0:tok, :] = jnp.where((lane < 64) | chosen, prob, -1.0)
 
     pl.semaphore_wait(barrier, len(others))
+    start_w(unroll, local_exp, slice(0, 2))
 
     def block(chip, o):
         return pl.ds((2 * chip + o) * tok, tok)
@@ -97,8 +102,17 @@
 
     partner = device_of(OWN, 1)
     to_partner = gather(0, block(OWN, 0), block(OWN, 1), partner)
-    to_chip = {chip: gather(chip, block(OWN, 0), block(chip, 0), device_of(chip, 0)) for chip in (DIAG, XN, YN)}
+    to_chip = {chip: gather(chip, block(OWN, 0), block(chip, 0), device_of(chip, 0)) for chip in (XN, YN)}
     forward = {chip: gather(3 + chip, block(chip, 0), block(chip, 1), partner) for chip in (DIAG, XN, YN)}
+    half = tok // 2
+
+    def half_of(chip, h):
+        return pl.ds(2 * chip * tok + h * half, half)
+
+    relay = {
+        YN: gather(1, half_of(YN, 1), half_of(DIAG, 1), device_of(XN, 0)),
+        XN: gather(7, half_of(XN, 0), half_of(DIAG, 0), device_of(YN, 0)),
+    }
 
     def start(copies):
         for c in copies:
@@ -108,17 +122,17 @@
         for c in copies:
             c.wait_recv()
 
-    def send_part(k):
+    for k in range(2):
         for copies in (to_partner, to_chip[XN], to_chip[YN]):
             copies[k].start()
-
-    send_part(0)
-    send_part(1)
-
-    def pass_on(chip, parts):
-        for k in parts:
-            to_chip[chip][k].wait_recv()
-            forward[chip][k].start()
+    to_partner[2].start()
+
+    def pass_on(parts):
+        for chip in (XN, YN):
+            for k in parts:
+                to_chip[chip][k].wait_recv()
+                relay[chip][k].start()
+                forward[chip][k].start()
 
     def cols_of(e):
         return pl.ds(pl.multiple_of(e * ffn, ffn), ffn)
@@ -126,8 +140,6 @@
     def gate_of(rows, count, e):
         lanes = lax.broadcasted_iota(jnp.int32, (count, LANES), 1)
         return jnp.sum(jnp.where(lanes == 64 + ep * GROUP + e, rt[rows, :], 0.0), axis=1, keepdims=True)
-
-    unroll = 5
 
     def over_experts(lo, hi, one, which=None):
         def body(i, carry):
@@ -159,8 +171,10 @@
 
         over_experts(lo, hi, one, slice(0, 2) if first else None)
 
-    def dy_pass(row, count, first=False):
+    def dy_pass(row, count, lo, hi):
         rows = pl.ds(row, count)
+        if lo == 0:
+            dgacc[...] = jnp.zeros_like(dgacc)
 
         def one(e):
             cols = cols_of(e)
@@ -174,13 +188,12 @@
             silu = h1 * sig
             act = (silu * h3).astype(BF16).astype(F32)
             dgate = jnp.sum(act * da, axis=1, keepdims=True)
-            dgacc[...] = jnp.where(lanes == ep * GROUP + e, dgate, dgacc[...])
+            dgacc[0:count, :] = jnp.where(lanes == ep * GROUP + e, dgate, dgacc[0:count, :])
             da = (gate * da).astype(BF16).astype(F32)
             d1[rows, cols] = jnp.where(on, da * (h3 * (sig * (1.0 + h1 * (1.0 - sig)))), 0.0).astype(BF16)
             d3[rows, cols] = jnp.where(on, da * silu, 0.0).astype(BF16)
 
-        dgacc[...] = jnp.zeros_like(dgacc)
-        over_experts(0, local_exp, one, slice(2, 3) if first else None)
+        over_experts(lo, hi, one)
 
     outs = []
 
@@ -206,64 +219,78 @@
                 if (chip, o) != (OWN, 0):
                     dg_copies[(chip, o)].start()
 
-    def sums_pass(row, chips, lo, hi):
-        rows = pl.ds(row, 4 * tok)
+    def sums_pass(row, chips, k, lo, hi):
+        rows = pl.ds(row, 2 * tok * len(chips))
         width = 256
         for n in range(lo, hi):
             cols = pl.ds(n * width, width)
-            y = dot(ga[rows, :], w2[:, cols])
-            dx = dot_t(d1[rows, :], w1[cols, :]) + dot_t(d3[rows, :], w3[cols, :])
-            for k, tile in enumerate((y, dx)):
-                for i, chip in enumerate(chips):
-                    at = 2 * tok * i
-                    ys[chip, k, :, cols] = tile[at : at + tok]
-                    yo[chip, k, :, cols] = tile[at + tok : at + 2 * tok].astype(BF16)
-
-    pair = [
-        pltpu.make_async_remote_copy(yo.at[pl.ds(2 * i, 2)], yr.at[pl.ds(2 * i, 2)], pair_send.at[i], pair_recv.at[i], device_id=partner, device_id_type=MESH)
-        for i in (0, 1)
-    ]
-    xy = [
-        pltpu.make_async_remote_copy(xs.at[i], xr.at[i], xy_send.at[i], xy_recv.at[i], device_id=device_of(chip, 0), device_id_type=MESH)
-        for i, chip in enumerate((XN, YN))
-    ]
+            tile = dot(ga[rows, :], w2[:, cols]) if k == 0 else dot_t(d1[rows, :], w1[cols, :]) + dot_t(d3[rows, :], w3[cols, :])
+            for i, chip in enumerate(chips):
+                at = 2 * tok * i
+                ys[chip, k, :, cols] = tile[at : at + tok]
+                yo[chip, k, :, cols] = tile[at + tok : at + 2 * tok].astype(BF16)
+
+    pair = {
+        (first, k): pltpu.make_async_remote_copy(
+            yo.at[pl.ds(first, 2), k], yr.at[pl.ds(first, 2), k], pair_send.at[first + k], pair_recv.at[first + k], device_id=partner, device_id_type=MESH
+        )
+        for first in (OWN, XN)
+        for k in (0, 1)
+    }
+    xy = {
+        (chip, k): pltpu.make_async_remote_copy(
+            xs.at[chip - XN, k], xr.at[chip - XN, k], xy_send.at[chip - XN, k], xy_recv.at[chip - XN, k], device_id=device_of(chip, 0), device_id_type=MESH
+        )
+        for chip in (XN, YN)
+        for k in (0, 1)
+    }
+
+    def send_xy(k):
+        pair[(XN, k)].wait_recv()
+        for chip in (XN, YN):
+            xs[chip - XN, k] = (ys[chip, k] + yr[chip, k].astype(F32)).astype(BF16)
+            xy[(chip, k)].start()
+
     steps = d_model // 256
 
     wait_recv(to_partner[:2])
-    u_pass(0, 2 * tok, 0, local_exp, first=True)
-    send_part(2)
-
-    for chip in (XN, YN):
-        pass_on(chip, (0, 1))
+    u_pass(0, 2 * tok, 0, unroll, first=True)
+    start_w(0, local_exp, slice(2, 3))
+    u_pass(0, 2 * tok, unroll, local_exp, first=True)
+    to_chip[XN][2].start()
+    to_chip[YN][2].start()
+    pass_on((0, 1))
+    for e in range(local_exp):
+        load_w(e)[2].wait()
+    sums_pass(0, (OWN,), 0, 0, steps)
+
     for chip in (XN, YN):
         wait_recv(forward[chip][:2])
-    u_pass(4 * tok, 4 * tok, 0, unroll)
-    start(to_chip[DIAG])
-    for chip in (XN, YN):
-        pass_on(chip, (2,))
-    u_pass(4 * tok, 4 * tok, unroll, local_exp)
+    u_pass(4 * tok, 4 * tok, 0, local_exp)
+    pass_on((2,))
+    sums_pass(4 * tok, (XN, YN), 0, 0, steps)
+    pair[(XN, 0)].start()
     for chip in (XN, YN):
         forward[chip][2].wait_recv()
-    dy_pass(4 * tok, 4 * tok, first=True)
+    dy_pass(4 * tok, 4 * tok, 0, unroll)
+    for k in range(3):
+        for copies in relay.values():
+            copies[k].wait_recv()
+        forward[DIAG][k].start()
+    send_xy(0)
+    dy_pass(4 * tok, 4 * tok, unroll, local_exp)
     write_out(4 * tok, 4 * tok, grads, 0)
     send_gates((XN, YN))
-    sums_pass(4 * tok, (XN, YN), 0, steps - 2)
-    pass_on(DIAG, (0, 1, 2))
-    sums_pass(4 * tok, (XN, YN), steps - 2, steps)
-    pair[1].start()
 
     wait_recv(forward[DIAG])
+    u_pass(2 * tok, 2 * tok, 0, local_exp)
     to_partner[2].wait_recv()
-    u_pass(2 * tok, 2 * tok, 0, local_exp)
-    pair[1].wait_recv()
-    for i, chip in enumerate((XN, YN)):
-        for k in (0, 1):
-            xs[i, k] = (ys[chip, k] + yr[chip, k].astype(F32)).astype(BF16)
-        xy[i].start()
-    dy_pass(0, 4 * tok)
+    dy_pass(0, 4 * tok, 0, local_exp)
     write_out(0, 4 * tok, grads, 1)
     send_gates((OWN, DIAG))
-    sums_pass(0, (OWN, DIAG), 0, steps - 2)
+
+    sums_pass(4 * tok, (XN, YN), 1, 0, steps)
+    pair[(XN, 1)].start()
 
     for c in dg_copies.values():
         c.wait_recv()
@@ -280,19 +307,24 @@
     dlb[0] = jnp.where(left, high.astype(F32), pltpu.roll(low, 64, 1)).astype(BF16)
     start(dl_copies.values())
 
-    sums_pass(0, (OWN, DIAG), steps - 2, steps)
-    pair[0].start()
+    sums_pass(2 * tok, (DIAG,), 0, 0, steps)
+    pair[(OWN, 0)].start()
+    send_xy(1)
+    sums_pass(0, (OWN, DIAG), 1, 0, steps)
+    pair[(OWN, 1)].start()
     du_router = dot(dlb[0], wr16[...])
     wait_recv(dl_copies.values())
     dl_out[...] = dlb[...].reshape(8 * tok, LANES)
-    pair[0].wait_recv()
-    for k in (0, 1):
+    for k, base in enumerate((u[0:tok, :].astype(F32), dy[0:tok, :].astype(F32) + du_router)):
+        pair[(OWN, k)].wait_recv()
         send_out[k] = (ys[DIAG, k] + yr[DIAG, k].astype(F32)).astype(BF16)
-    wait_recv(xy)
-    for k, base in enumerate((u[0:tok, :].astype(F32), dy[0:tok, :].astype(F32) + du_router)):
-        own_out[k] = ys[OWN, k] + yr[OWN, k].astype(F32) + base + xr[0, k].astype(F32) + xr[1, k].astype(F32)
-
-    for copies in (to_partner, *to_chip.values(), *forward.values(), dg_copies.values(), dl_copies.values(), pair, xy):
+        own = ys[OWN, k] + yr[OWN, k].astype(F32) + base
+        for chip in (XN, YN):
+            xy[(chip, k)].wait_recv()
+            own = own + xr[chip - XN, k].astype(F32)
+        own_out[k] = own
+
+    for copies in (to_partner, *to_chip.values(), *forward.values(), *relay.values(), dg_copies.values(), dl_copies.values(), pair.values(), xy.values()):
         for c in copies:
             c.wait_send()
     for c in outs:
@@ -356,8 +388,8 @@
                 pltpu.VMEM((8, tok, LANES), F32), pltpu.VMEM((8, tok, LANES), F32),
                 pltpu.VMEM((8, tok, LANES), BF16),
                 pltpu.VMEM((LANES, d_model), BF16),
-                dma((2,)), dma((3, local_exp)), dma((3, 7)), dma((3, 7)), dma((16,)), dma((16,)),
-                dma((2,)), dma((2,)), dma((2,)), dma((2,)), dma((2, 5)),
+                dma((2,)), dma((3, local_exp)), dma((3, 8)), dma((3, 8)), dma((16,)), dma((16,)),
+                dma((4,)), dma((4,)), dma((2, 2)), dma((2, 2)), dma((2, 5)),
             ],
             compiler_params=pltpu.CompilerParams(collective_id=0, has_side_effects=True, vmem_limit_bytes=62 * 1024 * 1024),
         )(u_loc, dy_loc, ids_loc.T, w_router.T, w_gate, w_up, w_down)

time: 75.3 us -> 70.1 us (0.931)
  Pallas kernels: 71.5 us -> 66.8 us
    pallas_call x1, Pallas kernels: 50.6 us -> 45.9 us  [device_step(): pl.pallas_call(functools.partial(rows_kernel, (tok, d_model, ffn, local_e...]
  transfers between devices with their start and end apart: 1 -> 1, of which waited for: 0 -> 0; matrix products, arithmetic and copies ran while one was open for 0% -> 0% of each run, Pallas kernels for 28% -> 30%
where the time goes in v3:
time: 70.1 us; the launch traced here: 69.7 us
  Pallas kernels  66.8 us (95%)
  starting transfers between devices  1.44 us (2%)
  other arithmetic  0.81 us (1%)
    pallas_call x1, Pallas kernels, device_step(): pl.pallas_call(functools.partial(rows_kernel, (tok, d_model, ffn, local_e...  45.9 us
    pallas_call x1, Pallas kernels, device_step(): pl.pallas_call(functools.partial(grads_kernel, local_exp), name='weight_g...  20.9 us
    ppermute x1, starting transfers between devices, device_step(): lax.ppermute(send, ('etp', 'ep'), [(i, i ^ n_ep + 2) for i in range(n_ep...  1.44 us
  transfers between devices with their start and end apart: 1, of which 0 were waited for; matrix products, arithmetic and copies ran while one was open for 0% of the time, Pallas kernels for 30%

profile of v3, /device:TPU:0, one launch (start us, length us, event | category | flops | bytes accessed | tf_op | source)
XLA Modules:
  0.0 69.7 jit_solution(16671803824989644069)
XLA Ops:
  0.6 45.9 %expert_rows.1 = (bf16[512,1536]{1,0:T(8,128)(2,1)}, bf16[512,1536]{1,0:T(8,128)(2,1)}, bf16[512,2560]{1,0:T(8,128)(2,1)}, bf16[512,2560]{1,0:T(8,128)(2,1)}, bf...) custom-call(bf16[64,1536]{1,0:T(8,128)(2,1)} %u_hbm.1, ...), custom_call_target="tpu_custom_call" | custom-call | tf_op jit(solution)/shard_map/expert_rows/pallas_call | solution.py:369
  46.6 1.4 %collective-permute-start = (bf16[2,64,1536]{2,1,0:T(8,128)(2,1)}, bf16[2,64,1536]{2,1,0:T(8,128)(2,1)S(1)}, u32[]{:S(2)}, u32[]{:S(2)}) collective-permute-start(bf16[2,64,1536]{2,1,0:T(8,128)(2,1)} %get-tuple-element.19), channel_id=1, source_target_pairs={{0,6},{1,7},{2,4},{3,5},{4,2},{5,3},{6,0},{7,1}} | collective-permute-start | bytes 1179656 | tf_op jit(solution)/shard_map/ppermute | solution.py:398
  48.0 0.0 copy-start
  48.0 20.9 %weight_grads.1 = (f32[10,1536,256]{2,1,0:T(8,128)}, f32[10,1536,256]{2,1,0:T(8,128)}, f32[10,256,1536]{2,1,0:T(8,128)}, f32[40,1536]{1,0:T(8,128)}) custom-call(bf16[512,1536]{1,0:T(8,128)(2,1)} %get-tuple-element.20.u_ref, bf16[512,1536]{1,0:T(8,128)(2,1)} %get-tuple-element.21.dy_ref, bf16[512,2560]{1,0:T(8,128)(2,1)} %get-tuple-element.22.ga_ref, ...), custom_call_target="tpu_custom_call" | custom-call | flops 12079595520 | bytes 60293120 | tf_op jit(solution)/shard_map/weight_grads/pallas_call | solution.py:402
  68.9 0.0 collective-permute-done
  68.9 0.0 copy-done
  68.9 0.8 %fusion.1 = (bf16[64,1536]{1,0:T(8,128)(2,1)}, bf16[64,1536]{1,0:T(8,128)(2,1)}) fusion(f32[2,64,1536]{2,1,0:T(8,128)S(1)} %copy-done, bf16[2,64,1536]{2,1,0:T(8,128)(2,1)S(1)} %collective-permute-done), kind=kLoop, calls=%fused_computation.3 | loop fusion | flops 589824 | bytes 1572864 | tf_op jit(solution)/shard_map/convert_element_type | solution.py:420
Async XLA Ops:
  46.6 22.3 %collective-permute-start = (bf16[2,64,1536]{2,1,0:T(8,128)(2,1)}, bf16[2,64,1536]{2,1,0:T(8,128)(2,1)S(1)}, u32[]{:S(2)}, u32[]{:S(2)}) collective-permute-start(bf16[2,64,1536]{2,1,0:T(8,128)(2,1)} %get-tuple-element.19), channel_id=1, source_target_pairs={{0,6},{1,7},{2,4},{3,5},{4,2},{5,3},{6,0},{7,1}} | collective-permute-start | bytes 1179656 | tf_op jit(solution)/shard_map/ppermute | solution.py:398
  48.0 20.9 %copy-start = (f32[2,64,1536]{2,1,0:T(8,128)S(1)}, f32[2,64,1536]{2,1,0:T(8,128)}, u32[]{:S(2)}) copy-start(f32[2,64,1536]{2,1,0:T(8,128)} %get-tuple-element.18) | copy-start | bytes 2359300

commit v4 on v3

--- a/solution.py
+++ b/solution.py
@@ -35,9 +35,9 @@
 
 def rows_kernel(
     sizes, u_hbm, dy_hbm, ids_ref, wr_ref, wg_hbm, wu_hbm, wd_hbm,
-    u_out, dy_out, ga_out, d1_out, d3_out, dl_out, own_out, send_out,
-    u, dy, rt, w1, w3, w2, ga, d1, d3, sg, ys, yo, yr, xs, xr, dgacc, dgb, dgr, dlb, wr16,
-    in_sem, w_sem, ag_send, ag_recv, small_send, small_recv, pair_send, pair_recv, xy_send, xy_recv, out_sem,
+    dy, ga, d1, d3, xt, dl_out, own_out, send_out,
+    u, rt, w1, w3, w2, sg, ys, yo, yr, xs, xr, dgacc, dgb, dgr, dlb, wr16,
+    in_sem, w_sem, ag_send, ag_recv, small_send, small_recv, pair_send, pair_recv, xy_send, xy_recv,
 ):
     tok, d_model, ffn, local_exp, experts, top_k = sizes
     ep = lax.axis_index("ep")
@@ -195,16 +195,6 @@
 
         over_experts(lo, hi, one)
 
-    outs = []
-
-    def write_out(row, count, pairs, sem):
-        rows = pl.ds(row, count)
-        copies = [pltpu.make_async_copy(s.at[rows, :], d.at[rows, :], out_sem.at[sem, k]) for k, (s, d) in enumerate(pairs)]
-        start(copies)
-        outs.extend(copies)
-
-    grads = ((ga, ga_out), (d1, d1_out), (d3, d3_out), (u, u_out), (dy, dy_out))
-
     def small(i, src, dst, dev):
         return pltpu.make_async_remote_copy(src, dst, small_send.at[i], small_recv.at[i], device_id=dev, device_id_type=MESH)
 
@@ -219,12 +209,14 @@
                 if (chip, o) != (OWN, 0):
                     dg_copies[(chip, o)].start()
 
-    def sums_pass(row, chips, k, lo, hi):
+    def sums_pass(row, chips, k, lo, hi, transpose=False):
         rows = pl.ds(row, 2 * tok * len(chips))
         width = 256
         for n in range(lo, hi):
             cols = pl.ds(n * width, width)
             tile = dot(ga[rows, :], w2[:, cols]) if k == 0 else dot_t(d1[rows, :], w1[cols, :]) + dot_t(d3[rows, :], w3[cols, :])
+            if transpose:
+                xt[cols, :] = u[:, cols].T
             for i, chip in enumerate(chips):
                 at = 2 * tok * i
                 ys[chip, k, :, cols] = tile[at : at + tok]
@@ -279,17 +271,15 @@
         forward[DIAG][k].start()
     send_xy(0)
     dy_pass(4 * tok, 4 * tok, unroll, local_exp)
-    write_out(4 * tok, 4 * tok, grads, 0)
     send_gates((XN, YN))
 
     wait_recv(forward[DIAG])
     u_pass(2 * tok, 2 * tok, 0, local_exp)
     to_partner[2].wait_recv()
     dy_pass(0, 4 * tok, 0, local_exp)
-    write_out(0, 4 * tok, grads, 1)
     send_gates((OWN, DIAG))
 
-    sums_pass(4 * tok, (XN, YN), 1, 0, steps)
+    sums_pass(4 * tok, (XN, YN), 1, 0, steps, transpose=True)
     pair[(XN, 1)].start()
 
     for c in dg_copies.values():
@@ -327,25 +317,45 @@
     for copies in (to_partner, *to_chip.values(), *forward.values(), *relay.values(), dg_copies.values(), dl_copies.values(), pair.values(), xy.values()):
         for c in copies:
             c.wait_send()
-    for c in outs:
-        c.wait()
-
-
-def grads_kernel(local_exp, u_ref, dy_ref, ga_ref, d1_ref, d3_ref, dl_ref, dwg_ref, dwu_ref, dwd_ref, dwr_ref, xt):
-    def over_tokens(a, b):
-        return lax.dot_general(a, b, (((0,), (0,)), ((), ())), preferred_element_type=F32)
-
-    @pl.when(pl.program_id(0) == 0)
-    def _():
-        xt[...] = u_ref[...].T
-        wide = over_tokens(dl_ref[...], u_ref[...])
-        wide = wide[0:64] + wide[64:128]
-        for g in range(dwr_ref.shape[0] // local_exp):
-            dwr_ref[g * local_exp : (g + 1) * local_exp, :] = wide[g * GROUP : g * GROUP + local_exp]
-
-    dwg_ref[0] = dot(xt[...], d1_ref[...])
-    dwu_ref[0] = dot(xt[...], d3_ref[...])
-    dwd_ref[0] = over_tokens(ga_ref[...], dy_ref[...])
+
+
+def grads_kernel(sizes, xt, dy, ga, d1, d3, dl, dwg_hbm, dwu_hbm, dwd_hbm, dwr_ref, gu, dn, sems):
+    local_exp, ffn = sizes
+
+    def copies(e, slot):
+        return [
+            pltpu.make_async_copy(gu.at[slot, :, pl.ds(0, ffn)], dwg_hbm.at[e], sems.at[0, slot]),
+            pltpu.make_async_copy(gu.at[slot, :, pl.ds(ffn, ffn)], dwu_hbm.at[e], sems.at[1, slot]),
+            pltpu.make_async_copy(dn.at[slot], dwd_hbm.at[e], sems.at[2, slot]),
+        ]
+
+    def one(e, slot):
+        cols = pl.ds(pl.multiple_of(e * ffn, ffn), ffn)
+        gu[slot] = dot(xt[...], jnp.concatenate([d1[:, cols], d3[:, cols]], axis=1))
+        for c in copies(e, slot)[:2]:
+            c.start()
+        dn[slot] = lax.dot_general(ga[:, cols], dy[...], (((0,), (0,)), ((), ())), preferred_element_type=F32)
+        copies(e, slot)[2].start()
+
+    def body(i, carry):
+        for slot in (0, 1):
+
+            @pl.when(i > 0)
+            def _():
+                for c in copies(2 * i + slot - 2, slot):
+                    c.wait()
+
+            one(2 * i + slot, slot)
+        return carry
+
+    lax.fori_loop(0, local_exp // 2, body, 0)
+    wide = dot_t(dl[...].T, xt[...])
+    wide = wide[0:64] + wide[64:128]
+    for g in range(dwr_ref.shape[0] // local_exp):
+        dwr_ref[g * local_exp : (g + 1) * local_exp, :] = wide[g * GROUP : g * GROUP + local_exp]
+    for slot in (0, 1):
+        for c in copies(local_exp - 2 + slot, slot):
+            c.wait()
 
 
 def solution(mesh):
@@ -366,21 +376,22 @@
         vmem_spec = pl.BlockSpec(memory_space=pltpu.VMEM)
         S = jax.ShapeDtypeStruct
         dma = pltpu.SemaphoreType.DMA
-        u, dy, ga, d1, d3, dl, own, send = pl.pallas_call(
+        dy, ga, d1, d3, xt, dl, own, send = pl.pallas_call(
             functools.partial(rows_kernel, (tok, d_model, ffn, local_exp, experts, top_k)),
             name="expert_rows",
             in_specs=[any_spec, any_spec, vmem_spec, vmem_spec, any_spec, any_spec, any_spec],
-            out_specs=[any_spec] * 5 + [vmem_spec] * 3,
+            out_specs=[vmem_spec] * 8,
             out_shape=[
-                S((rows, d_model), BF16), S((rows, d_model), BF16),
-                S((rows, wide), BF16), S((rows, wide), BF16), S((rows, wide), BF16),
-                S((rows, LANES), BF16), S((2, tok, d_model), F32), S((2, tok, d_model), BF16),
+                pltpu.VMEM((rows, d_model), BF16),
+                pltpu.VMEM((rows, wide), BF16), pltpu.VMEM((rows, wide), BF16), pltpu.VMEM((rows, wide), BF16),
+                pltpu.VMEM((d_model, rows), BF16), pltpu.VMEM((rows, LANES), BF16),
+                S((2, tok, d_model), F32), S((2, tok, d_model), BF16),
             ],
             scratch_shapes=[
-                pltpu.VMEM((rows, d_model), BF16), pltpu.VMEM((rows, d_model), BF16),
+                pltpu.VMEM((rows, d_model), BF16),
                 pltpu.VMEM((rows, LANES), F32),
                 pltpu.VMEM((d_model, wide), BF16), pltpu.VMEM((d_model, wide), BF16), pltpu.VMEM((wide, d_model), BF16),
-                pltpu.VMEM((rows, wide), BF16), pltpu.VMEM((rows, wide), BF16), pltpu.VMEM((rows, wide), BF16), pltpu.VMEM((rows, wide), F32),
+                pltpu.VMEM((rows, wide), F32),
                 pltpu.VMEM((4, 2, tok, d_model), F32),
                 pltpu.VMEM((4, 2, tok, d_model), BF16), pltpu.VMEM((4, 2, tok, d_model), BF16),
                 pltpu.VMEM((2, 2, tok, d_model), BF16), pltpu.VMEM((2, 2, tok, d_model), BF16),
@@ -389,32 +400,25 @@
                 pltpu.VMEM((8, tok, LANES), BF16),
                 pltpu.VMEM((LANES, d_model), BF16),
                 dma((2,)), dma((3, local_exp)), dma((3, 8)), dma((3, 8)), dma((16,)), dma((16,)),
-                dma((4,)), dma((4,)), dma((2, 2)), dma((2, 2)), dma((2, 5)),
+                dma((4,)), dma((4,)), dma((2, 2)), dma((2, 2)),
             ],
-            compiler_params=pltpu.CompilerParams(collective_id=0, has_side_effects=True, vmem_limit_bytes=62 * 1024 * 1024),
+            compiler_params=pltpu.CompilerParams(collective_id=0, has_side_effects=True, vmem_limit_bytes=48 * 1024 * 1024),
         )(u_loc, dy_loc, ids_loc.T, w_router.T, w_gate, w_up, w_down)
 
         n_ep, n_etp = lax.axis_size("ep"), lax.axis_size("etp")
         got = lax.ppermute(send, ("etp", "ep"), [(i, i ^ (n_ep + 2)) for i in range(n_ep * n_etp)])
 
-        col_block = pl.BlockSpec((rows, ffn), lambda e: (0, e))
-        whole_rows = pl.BlockSpec((rows, d_model), lambda e: (0, 0))
+        kept = [pltpu.with_memory_space_constraint(a, pltpu.VMEM) for a in (xt, dy, ga, d1, d3, dl)]
         dwg, dwu, dwd, dwr = pl.pallas_call(
-            functools.partial(grads_kernel, local_exp),
+            functools.partial(grads_kernel, (local_exp, ffn)),
             name="weight_grads",
-            grid=(local_exp,),
-            in_specs=[whole_rows, whole_rows, col_block, col_block, col_block, pl.BlockSpec((rows, LANES), lambda e: (0, 0))],
-            out_specs=[
-                pl.BlockSpec((1, d_model, ffn), lambda e: (e, 0, 0)),
-                pl.BlockSpec((1, d_model, ffn), lambda e: (e, 0, 0)),
-                pl.BlockSpec((1, ffn, d_model), lambda e: (e, 0, 0)),
-                pl.BlockSpec((experts, d_model), lambda e: (0, 0)),
-            ],
+            in_specs=[vmem_spec] * 6,
+            out_specs=[any_spec] * 3 + [vmem_spec],
             out_shape=[S((local_exp, d_model, ffn), F32), S((local_exp, d_model, ffn), F32), S((local_exp, ffn, d_model), F32), S((experts, d_model), F32)],
-            scratch_shapes=[pltpu.VMEM((d_model, rows), BF16)],
-            compiler_params=pltpu.CompilerParams(vmem_limit_bytes=62 * 1024 * 1024),
+            scratch_shapes=[pltpu.VMEM((2, d_model, 2 * ffn), F32), pltpu.VMEM((2, ffn, d_model), F32), dma((3, 2))],
+            compiler_params=pltpu.CompilerParams(vmem_limit_bytes=24 * 1024 * 1024),
             cost_estimate=pl.CostEstimate(flops=3 * 2 * rows * wide * d_model, bytes_accessed=12 * wide * d_model + 10 * rows * wide, transcendentals=0),
-        )(u, dy, ga, d1, d3, dl)
+        )(*kept)
 
         y_loc = (own[0] + got[0].astype(F32)).astype(BF16)
         du_loc = (own[1] + got[1].astype(F32)).astype(BF16)

time: 70.1 us -> 66.5 us (0.949)
  Pallas kernels: 66.8 us -> 63.5 us
    pallas_call x1, Pallas kernels: 20.9 us -> 17.7 us  [device_step(): pl.pallas_call(functools.partial(grads_kernel, (local_exp, ffn)), name='w...]
  transfers between devices with their start and end apart: 1 -> 1, of which waited for: 0 -> 0; matrix products, arithmetic and copies ran while one was open for 0% -> 0% of each run, Pallas kernels for 30% -> 27%
where the time goes in v4:
time: 66.5 us; the launch traced here: 66.4 us
  Pallas kernels  63.5 us (95%)
  starting transfers between devices  1.43 us (2%)
  other arithmetic  0.81 us (1%)
  between operations  0.67 us (1%)
    pallas_call x1, Pallas kernels, device_step(): pl.pallas_call(functools.partial(rows_kernel, (tok, d_model, ffn, local_e...  45.8 us
    pallas_call x1, Pallas kernels, device_step(): pl.pallas_call(functools.partial(grads_kernel, (local_exp, ffn)), name='w...  17.7 us
    ppermute x1, starting transfers between devices, device_step(): lax.ppermute(send, ('etp', 'ep'), [(i, i ^ n_ep + 2) for i in range(n_ep...  1.43 us
  transfers between devices with their start and end apart: 1, of which 0 were waited for; matrix products, arithmetic and copies ran while one was open for 0% of the time, Pallas kernels for 27%

profile of v4, /device:TPU:0, one launch (start us, length us, event | category | flops | bytes accessed | tf_op | source)
XLA Modules:
  0.0 66.4 jit_solution(1615304241756201691)
XLA Ops:
  0.6 45.8 %expert_rows.1 = (bf16[512,1536]{1,0:T(8,128)(2,1)S(1)}, bf16[512,2560]{1,0:T(8,128)(2,1)S(1)}, bf16[512,2560]{1,0:T(8,128)(2,1)S(1)}, bf16[512,2560]{1,0:T(8,12...) custom-call(bf16[64,1536]{1,0:T(8,128)(2,1)} %u_hbm.1, ...), custom_call_target="tpu_custom_call" | custom-call | tf_op jit(solution)/shard_map/expert_rows/pallas_call | solution.py:379
  46.4 1.4 %collective-permute-start = (bf16[2,64,1536]{2,1,0:T(8,128)(2,1)}, bf16[2,64,1536]{2,1,0:T(8,128)(2,1)S(1)}, u32[]{:S(2)}, u32[]{:S(2)}) collective-permute-start(bf16[2,64,1536]{2,1,0:T(8,128)(2,1)} %get-tuple-element.19), channel_id=1, source_target_pairs={{0,6},{1,7},{2,4},{3,5},{4,2},{5,3},{6,0},{7,1}} | collective-permute-start | bytes 1179656 | tf_op jit(solution)/shard_map/ppermute | solution.py:409
  47.9 0.0 copy-start
  47.9 17.7 %weight_grads.1 = (f32[10,1536,256]{2,1,0:T(8,128)}, f32[10,1536,256]{2,1,0:T(8,128)}, f32[10,256,1536]{2,1,0:T(8,128)}, f32[40,1536]{1,0:T(8,128)}) custom-call(bf16[1536,512]{1,0:T(8,128)(2,1)S(1)} %get-tuple-element.20.xt, bf16[512,1536]{1,0:T(8,128)(2,1)S(1)} %get-tuple-element.21.dy, bf16[512,2560]{1,0:T(8,128)(2,1)S(1)} %get-tuple-element.22.ga, ...), custom_call_target="tpu_custom_call" | custom-call | flops 12079595520 | bytes 60293120 | tf_op jit(solution)/shard_map/weight_grads/pallas_call | solution.py:412
  65.6 0.0 collective-permute-done
  65.6 0.0 copy-done
  65.6 0.8 %fusion.1 = (bf16[64,1536]{1,0:T(8,128)(2,1)}, bf16[64,1536]{1,0:T(8,128)(2,1)}) fusion(f32[2,64,1536]{2,1,0:T(8,128)S(1)} %copy-done, bf16[2,64,1536]{2,1,0:T(8,128)(2,1)S(1)} %collective-permute-done), kind=kLoop, calls=%fused_computation.3 | loop fusion | flops 589824 | bytes 1572864 | tf_op jit(solution)/shard_map/convert_element_type | solution.py:424
Async XLA Ops:
  46.4 19.1 %collective-permute-start = (bf16[2,64,1536]{2,1,0:T(8,128)(2,1)}, bf16[2,64,1536]{2,1,0:T(8,128)(2,1)S(1)}, u32[]{:S(2)}, u32[]{:S(2)}) collective-permute-start(bf16[2,64,1536]{2,1,0:T(8,128)(2,1)} %get-tuple-element.19), channel_id=1, source_target_pairs={{0,6},{1,7},{2,4},{3,5},{4,2},{5,3},{6,0},{7,1}} | collective-permute-start | bytes 1179656 | tf_op jit(solution)/shard_map/ppermute | solution.py:409
  47.9 17.7 %copy-start = (f32[2,64,1536]{2,1,0:T(8,128)S(1)}, f32[2,64,1536]{2,1,0:T(8,128)}, u32[]{:S(2)}) copy-start(f32[2,64,1536]{2,1,0:T(8,128)} %get-tuple-element.18) | copy-start | bytes 2359300

commit v5 on v4

--- a/solution.py
+++ b/solution.py
@@ -34,16 +34,17 @@
 
 
 def rows_kernel(
-    sizes, u_hbm, dy_hbm, ids_ref, wr_ref, wg_hbm, wu_hbm, wd_hbm,
+    sizes, u_hbm, dy_hbm, ids_hbm, wr_hbm, wg_hbm, wu_hbm, wd_hbm,
     dy, ga, d1, d3, xt, dl_out, own_out, send_out,
-    u, rt, w1, w3, w2, sg, ys, yo, yr, xs, xr, dgacc, dgb, dgr, dlb, wr16,
+    u, ids_ref, wr_ref, rt, w1, w3, w2, sg, das, ys, yo, yr, xs, xr, dgacc, dgb, dgr, dlb, wr16,
     in_sem, w_sem, ag_send, ag_recv, small_send, small_recv, pair_send, pair_recv, xy_send, xy_recv,
 ):
     tok, d_model, ffn, local_exp, experts, top_k = sizes
     ep = lax.axis_index("ep")
 
     load_rows = [pltpu.make_async_copy(src, dst.at[pl.ds(0, tok), :], in_sem.at[k]) for k, (src, dst) in enumerate(((u_hbm, u), (dy_hbm, dy)))]
-    for c in load_rows:
+    load_small = [pltpu.make_async_copy(src, dst, in_sem.at[2 + k]) for k, (src, dst) in enumerate(((wr_hbm, wr_ref), (ids_hbm, ids_ref)))]
+    for c in load_rows + load_small:
         c.start()
 
     def load_w(e):
@@ -54,14 +55,67 @@
             pltpu.make_async_copy(wd_hbm.at[e], w2.at[cols, :], w_sem.at[2, e]),
         ]
 
+    unroll = 5
+
+    def start_w(lo, hi, which):
+        for e in range(lo, hi):
+            for c in load_w(e)[which]:
+                c.start()
+
+    start_w(0, 1, slice(0, 2))
+
     barrier = pltpu.get_barrier_semaphore()
     others = [(chip, o) for chip in (OWN, DIAG, XN, YN) for o in (0, 1) if (chip, o) != (OWN, 0)]
     for chip, o in others:
         pl.semaphore_signal(barrier, inc=1, device_id=device_of(chip, o), device_id_type=MESH)
 
+    def block(chip, o):
+        return pl.ds((2 * chip + o) * tok, tok)
+
+    def gather(i, src, dst, dev):
+        return [
+            pltpu.make_async_remote_copy(ref.at[src, :], ref.at[dst, :], ag_send.at[k, i], ag_recv.at[k, i], device_id=dev, device_id_type=MESH)
+            for k, ref in enumerate((rt, u, dy))
+        ]
+
+    partner = device_of(OWN, 1)
+    to_partner = gather(0, block(OWN, 0), block(OWN, 1), partner)
+    to_chip = {chip: gather(chip, block(OWN, 0), block(chip, 0), device_of(chip, 0)) for chip in (XN, YN)}
+    forward = {chip: gather(3 + chip, block(chip, 0), block(chip, 1), partner) for chip in (DIAG, XN, YN)}
+    half = tok // 2
+
+    def half_of(chip, h):
+        return pl.ds(2 * chip * tok + h * half, half)
+
+    relay = {
+        YN: gather(1, half_of(YN, 1), half_of(DIAG, 1), device_of(XN, 0)),
+        XN: gather(7, half_of(XN, 0), half_of(DIAG, 0), device_of(YN, 0)),
+    }
+
+    def start(copies):
+        for c in copies:
+            c.start()
+
+    def wait_recv(copies):
+        for c in copies:
+            c.wait_recv()
+
+    def send_part(k, chips):
+        for copies in chips:
+            copies[k].start()
+
+    first_chips = (to_partner, to_chip[XN], to_chip[YN])
+    for c in load_rows:
+        c.wait()
+    start_w(1, local_exp, slice(0, 2))
+    pl.semaphore_wait(barrier, len(others))
+    send_part(1, first_chips)
+
     slot40 = lax.broadcasted_iota(jnp.int32, (LANES, experts), 0) % 64
     col40 = lax.broadcasted_iota(jnp.int32, (LANES, experts), 1)
     spread = (col40 == (slot40 // GROUP) * local_exp + slot40 % GROUP) & (slot40 % GROUP < local_exp)
+    for c in load_small:
+        c.wait()
     wr16[...] = dot(jnp.where(spread, 1.0, 0.0).astype(BF16), wr_ref[...]).astype(BF16)
     slot_t = lax.broadcasted_iota(jnp.int32, (LANES, tok), 0) % 64
     expert_t = jnp.where(slot_t % GROUP < local_exp, (slot_t // GROUP) * local_exp + slot_t % GROUP, -1)
@@ -71,60 +125,12 @@
     chosen = chosen_t.T > 0.5
     lane = lax.broadcasted_iota(jnp.int32, (tok, LANES), 1)
     valid = lane % GROUP < local_exp
-    for c in load_rows:
-        c.wait()
-    unroll = 5
-
-    def start_w(lo, hi, which):
-        for e in range(lo, hi):
-            for c in load_w(e)[which]:
-                c.start()
-
-    start_w(0, unroll, slice(0, 2))
-
     logits = jnp.where(valid, dot_t(u[0:tok, :], wr16[...]), -1e30)
     top = jnp.max(logits, axis=1, keepdims=True)
     expo = jnp.where(valid, jnp.exp(logits - top), 0.0)
     prob = expo / jnp.sum(jnp.where(lane < 64, expo, 0.0), axis=1, keepdims=True)
     rt[0:tok, :] = jnp.where((lane < 64) | chosen, prob, -1.0)
-
-    pl.semaphore_wait(barrier, len(others))
-    start_w(unroll, local_exp, slice(0, 2))
-
-    def block(chip, o):
-        return pl.ds((2 * chip + o) * tok, tok)
-
-    def gather(i, src, dst, dev):
-        return [
-            pltpu.make_async_remote_copy(ref.at[src, :], ref.at[dst, :], ag_send.at[k, i], ag_recv.at[k, i], device_id=dev, device_id_type=MESH)
-            for k, ref in enumerate((rt, u, dy))
-        ]
-
-    partner = device_of(OWN, 1)
-    to_partner = gather(0, block(OWN, 0), block(OWN, 1), partner)
-    to_chip = {chip: gather(chip, block(OWN, 0), block(chip, 0), device_of(chip, 0)) for chip in (XN, YN)}
-    forward = {chip: gather(3 + chip, block(chip, 0), block(chip, 1), partner) for chip in (DIAG, XN, YN)}
-    half = tok // 2
-
-    def half_of(chip, h):
-        return pl.ds(2 * chip * tok + h * half, half)
-
-    relay = {
-        YN: gather(1, half_of(YN, 1), half_of(DIAG, 1), device_of(XN, 0)),
-        XN: gather(7, half_of(XN, 0), half_of(DIAG, 0), device_of(YN, 0)),
-    }
-
-    def start(copies):
-        for c in copies:
-            c.start()
-
-    def wait_recv(copies):
-        for c in copies:
-            c.wait_recv()
-
-    for k in range(2):
-        for copies in (to_partner, to_chip[XN], to_chip[YN]):
-            copies[k].start()
+    send_part(0, first_chips)
     to_partner[2].start()
 
     def pass_on(parts):
@@ -148,7 +154,7 @@
                     for c in load_w(i * unroll + k)[which]:
                         c.wait()
             for k in range(unroll):
-                one(i * unroll + k)
+                one(i * unroll + k, k % 2)
             return carry
 
         lax.fori_loop(lo // unroll, hi // unroll, body, 0)
@@ -156,18 +162,19 @@
     def u_pass(row, count, lo, hi, first=False):
         rows = pl.ds(row, count)
 
-        def one(e):
+        def one(e, slot):
             cols = cols_of(e)
-            h1 = dot(u[rows, :], w1[:, cols]).astype(BF16)
-            h3 = dot(u[rows, :], w3[:, cols]).astype(BF16)
+            gate = gate_of(rows, count, e)
+            on = gate >= 0.0
+            h1 = jnp.where(on, dot(u[rows, :], w1[:, cols]), 0.0).astype(BF16)
+            h3 = jnp.where(on, dot(u[rows, :], w3[:, cols]), 0.0).astype(BF16)
             d1[rows, cols] = h1
             d3[rows, cols] = h3
-            gate = gate_of(rows, count, e)
             h1 = h1.astype(F32)
             sig = jax.nn.sigmoid(h1)
             sg[rows, cols] = sig
             act = (h1 * sig * h3.astype(F32)).astype(BF16).astype(F32)
-            ga[rows, cols] = jnp.where(gate >= 0.0, gate * act, 0.0).astype(BF16)
+            ga[rows, cols] = (gate * act).astype(BF16)
 
         over_experts(lo, hi, one, slice(0, 2) if first else None)
 
@@ -176,22 +183,24 @@
         if lo == 0:
             dgacc[...] = jnp.zeros_like(dgacc)
 
-        def one(e):
+        def one(e, slot):
             cols = cols_of(e)
-            da = dot_t(dy[rows, :], w2[cols, :])
-            lanes = lax.broadcasted_iota(jnp.int32, (count, LANES), 1)
-            gate = gate_of(rows, count, e)
-            on = gate >= 0.0
-            h1 = d1[rows, cols].astype(F32)
-            h3 = d3[rows, cols].astype(F32)
-            sig = sg[rows, cols]
-            silu = h1 * sig
-            act = (silu * h3).astype(BF16).astype(F32)
-            dgate = jnp.sum(act * da, axis=1, keepdims=True)
-            dgacc[0:count, :] = jnp.where(lanes == ep * GROUP + e, dgate, dgacc[0:count, :])
-            da = (gate * da).astype(BF16).astype(F32)
-            d1[rows, cols] = jnp.where(on, da * (h3 * (sig * (1.0 + h1 * (1.0 - sig)))), 0.0).astype(BF16)
-            d3[rows, cols] = jnp.where(on, da * silu, 0.0).astype(BF16)
+            das[slot, 0:count, :] = dot_t(dy[rows, :], w2[cols, :])
+            for at in range(0, count, tok):
+                part = pl.ds(row + at, tok)
+                lanes = lax.broadcasted_iota(jnp.int32, (tok, LANES), 1)
+                gate = gate_of(part, tok, e)
+                h1 = d1[part, cols].astype(F32)
+                h3 = d3[part, cols].astype(F32)
+                sig = sg[part, cols]
+                silu = h1 * sig
+                da = das[slot, at : at + tok, :]
+                act = (silu * h3).astype(BF16).astype(F32)
+                dgate = jnp.sum(act * da, axis=1, keepdims=True)
+                dgacc[at : at + tok, :] = jnp.where(lanes == ep * GROUP + e, dgate, dgacc[at : at + tok, :])
+                da = jnp.where(gate >= 0.0, gate * da, 0.0).astype(BF16).astype(F32)
+                d1[part, cols] = (da * h3 * (sig + silu - silu * sig)).astype(BF16)
+                d3[part, cols] = (da * silu).astype(BF16)
 
         over_experts(lo, hi, one)
 
@@ -222,28 +231,32 @@
                 ys[chip, k, :, cols] = tile[at : at + tok]
                 yo[chip, k, :, cols] = tile[at + tok : at + 2 * tok].astype(BF16)
 
+    steps = d_model // 256
+    early = 4
+    every, front, back = pl.ds(0, d_model), pl.ds(0, early * 256), pl.ds(early * 256, d_model - early * 256)
+    parts = {"xy y": (XN, 0, every), "xy dx 0": (XN, 1, front), "xy dx 1": (XN, 1, back), "od y": (OWN, 0, every), "od dx": (OWN, 1, every)}
     pair = {
-        (first, k): pltpu.make_async_remote_copy(
-            yo.at[pl.ds(first, 2), k], yr.at[pl.ds(first, 2), k], pair_send.at[first + k], pair_recv.at[first + k], device_id=partner, device_id_type=MESH
+        name: pltpu.make_async_remote_copy(
+            yo.at[pl.ds(first, 2), k, :, cols], yr.at[pl.ds(first, 2), k, :, cols], pair_send.at[i], pair_recv.at[i], device_id=partner, device_id_type=MESH
         )
-        for first in (OWN, XN)
-        for k in (0, 1)
+        for i, (name, (first, k, cols)) in enumerate(parts.items())
     }
     xy = {
-        (chip, k): pltpu.make_async_remote_copy(
-            xs.at[chip - XN, k], xr.at[chip - XN, k], xy_send.at[chip - XN, k], xy_recv.at[chip - XN, k], device_id=device_of(chip, 0), device_id_type=MESH
+        (name, chip): pltpu.make_async_remote_copy(
+            xs.at[chip - XN, k, :, cols], xr.at[chip - XN, k, :, cols], xy_send.at[chip - XN, i], xy_recv.at[chip - XN, i], device_id=device_of(chip, 0), device_id_type=MESH
         )
+        for i, (name, (first, k, cols)) in enumerate(parts.items())
+        if first == XN
         for chip in (XN, YN)
-        for k in (0, 1)
     }
 
-    def send_xy(k):
-        pair[(XN, k)].wait_recv()
+    def send_xy(name):
+        _, k, cols = parts[name]
+        pair[name].wait_recv()
         for chip in (XN, YN):
-            xs[chip - XN, k] = (ys[chip, k] + yr[chip, k].astype(F32)).astype(BF16)
-            xy[(chip, k)].start()
-
-    steps = d_model // 256
+            xs[chip - XN, k, :, cols] = (ys[chip, k, :, cols] + yr[chip, k, :, cols].astype(F32)).astype(BF16)
+            xy[(name, chip)].start()
+
 
     wait_recv(to_partner[:2])
     u_pass(0, 2 * tok, 0, unroll, first=True)
@@ -251,7 +264,7 @@
     u_pass(0, 2 * tok, unroll, local_exp, first=True)
     to_chip[XN][2].start()
     to_chip[YN][2].start()
-    pass_on((0, 1))
+    pass_on((1, 0))
     for e in range(local_exp):
         load_w(e)[2].wait()
     sums_pass(0, (OWN,), 0, 0, steps)
@@ -261,26 +274,38 @@
     u_pass(4 * tok, 4 * tok, 0, local_exp)
     pass_on((2,))
     sums_pass(4 * tok, (XN, YN), 0, 0, steps)
-    pair[(XN, 0)].start()
+    pair["xy y"].start()
     for chip in (XN, YN):
         forward[chip][2].wait_recv()
     dy_pass(4 * tok, 4 * tok, 0, unroll)
-    for k in range(3):
-        for copies in relay.values():
-            copies[k].wait_recv()
-        forward[DIAG][k].start()
-    send_xy(0)
+    def pass_on_diag(parts):
+        for k in parts:
+            for copies in relay.values():
+                copies[k].wait_recv()
+            forward[DIAG][k].start()
+
+    pass_on_diag((1, 0))
+    send_xy("xy y")
     dy_pass(4 * tok, 4 * tok, unroll, local_exp)
+    pass_on_diag((2,))
     send_gates((XN, YN))
-
-    wait_recv(forward[DIAG])
-    u_pass(2 * tok, 2 * tok, 0, local_exp)
+    sums_pass(4 * tok, (XN, YN), 1, 0, early)
+    pair["xy dx 0"].start()
+
+    wait_recv(forward[DIAG][:2])
+    u_pass(2 * tok, 2 * tok, 0, unroll)
+    send_xy("xy dx 0")
+    u_pass(2 * tok, 2 * tok, unroll, local_exp)
     to_partner[2].wait_recv()
+    forward[DIAG][2].wait_recv()
     dy_pass(0, 4 * tok, 0, local_exp)
     send_gates((OWN, DIAG))
 
-    sums_pass(4 * tok, (XN, YN), 1, 0, steps, transpose=True)
-    pair[(XN, 1)].start()
+    sums_pass(4 * tok, (XN, YN), 1, early, steps)
+    pair["xy dx 1"].start()
+    sums_pass(2 * tok, (DIAG,), 0, 0, steps)
+    pair["od y"].start()
+    send_xy("xy dx 1")
 
     for c in dg_copies.values():
         c.wait_recv()
@@ -297,22 +322,19 @@
     dlb[0] = jnp.where(left, high.astype(F32), pltpu.roll(low, 64, 1)).astype(BF16)
     start(dl_copies.values())
 
-    sums_pass(2 * tok, (DIAG,), 0, 0, steps)
-    pair[(OWN, 0)].start()
-    send_xy(1)
-    sums_pass(0, (OWN, DIAG), 1, 0, steps)
-    pair[(OWN, 1)].start()
+    sums_pass(0, (OWN, DIAG), 1, 0, steps, transpose=True)
+    pair["od dx"].start()
     du_router = dot(dlb[0], wr16[...])
     wait_recv(dl_copies.values())
     dl_out[...] = dlb[...].reshape(8 * tok, LANES)
     for k, base in enumerate((u[0:tok, :].astype(F32), dy[0:tok, :].astype(F32) + du_router)):
-        pair[(OWN, k)].wait_recv()
+        pair[("od y", "od dx")[k]].wait_recv()
         send_out[k] = (ys[DIAG, k] + yr[DIAG, k].astype(F32)).astype(BF16)
         own = ys[OWN, k] + yr[OWN, k].astype(F32) + base
-        for chip in (XN, YN):
-            xy[(chip, k)].wait_recv()
-            own = own + xr[chip - XN, k].astype(F32)
-        own_out[k] = own
+        for (name, chip), copy in xy.items():
+            if parts[name][1] == k:
+                copy.wait_recv()
+        own_out[k] = own + xr[0, k].astype(F32) + xr[1, k].astype(F32)
 
     for copies in (to_partner, *to_chip.values(), *forward.values(), *relay.values(), dg_copies.values(), dl_copies.values(), pair.values(), xy.values()):
         for c in copies:
@@ -379,19 +401,19 @@
         dy, ga, d1, d3, xt, dl, own, send = pl.pallas_call(
             functools.partial(rows_kernel, (tok, d_model, ffn, local_exp, experts, top_k)),
             name="expert_rows",
-            in_specs=[any_spec, any_spec, vmem_spec, vmem_spec, any_spec, any_spec, any_spec],
+            in_specs=[any_spec] * 7,
             out_specs=[vmem_spec] * 8,
             out_shape=[
                 pltpu.VMEM((rows, d_model), BF16),
                 pltpu.VMEM((rows, wide), BF16), pltpu.VMEM((rows, wide), BF16), pltpu.VMEM((rows, wide), BF16),
                 pltpu.VMEM((d_model, rows), BF16), pltpu.VMEM((rows, LANES), BF16),
-                S((2, tok, d_model), F32), S((2, tok, d_model), BF16),
+                pltpu.VMEM((2, tok, d_model), F32), pltpu.VMEM((2, tok, d_model), BF16),
             ],
             scratch_shapes=[
-                pltpu.VMEM((rows, d_model), BF16),
+                pltpu.VMEM((rows, d_model), BF16), pltpu.VMEM((top_k, tok), jnp.int32), pltpu.VMEM((experts, d_model), BF16),
                 pltpu.VMEM((rows, LANES), F32),
                 pltpu.VMEM((d_model, wide), BF16), pltpu.VMEM((d_model, wide), BF16), pltpu.VMEM((wide, d_model), BF16),
-                pltpu.VMEM((rows, wide), F32),
+                pltpu.VMEM((rows, wide), F32), pltpu.VMEM((2, 4 * tok, ffn), F32),
                 pltpu.VMEM((4, 2, tok, d_model), F32),
                 pltpu.VMEM((4, 2, tok, d_model), BF16), pltpu.VMEM((4, 2, tok, d_model), BF16),
                 pltpu.VMEM((2, 2, tok, d_model), BF16), pltpu.VMEM((2, 2, tok, d_model), BF16),
@@ -399,8 +421,8 @@
                 pltpu.VMEM((8, tok, LANES), F32), pltpu.VMEM((8, tok, LANES), F32),
                 pltpu.VMEM((8, tok, LANES), BF16),
                 pltpu.VMEM((LANES, d_model), BF16),
-                dma((2,)), dma((3, local_exp)), dma((3, 8)), dma((3, 8)), dma((16,)), dma((16,)),
-                dma((4,)), dma((4,)), dma((2, 2)), dma((2, 2)),
+                dma((4,)), dma((3, local_exp)), dma((3, 8)), dma((3, 8)), dma((16,)), dma((16,)),
+                dma((5,)), dma((5,)), dma((2, 3)), dma((2, 3)),
             ],
             compiler_params=pltpu.CompilerParams(collective_id=0, has_side_effects=True, vmem_limit_bytes=48 * 1024 * 1024),
         )(u_loc, dy_loc, ids_loc.T, w_router.T, w_gate, w_up, w_down)

time: 66.5 us -> 63.9 us (0.961)
  Pallas kernels: 63.5 us -> 61.3 us
    pallas_call x1, Pallas kernels: 45.8 us -> 43.6 us  [device_step(): pl.pallas_call(functools.partial(rows_kernel, (tok, d_model, ffn, local_e...]
  transfers between devices with their start and end apart: 1 -> 1, of which waited for: 0 -> 0; matrix products, arithmetic and copies ran while one was open for 0% -> 0% of each run, Pallas kernels for 27% -> 28%
where the time goes in v5:
time: 63.9 us; the launch traced here: 63.8 us
  Pallas kernels  61.3 us (96%)
  starting transfers between devices  0.94 us (1%)
  other arithmetic  0.81 us (1%)
  between operations  0.66 us (1%)
    pallas_call x1, Pallas kernels, device_step(): pl.pallas_call(functools.partial(rows_kernel, (tok, d_model, ffn, local_e...  43.6 us
    pallas_call x1, Pallas kernels, device_step(): pl.pallas_call(functools.partial(grads_kernel, (local_exp, ffn)), name='w...  17.7 us
  transfers between devices with their start and end apart: 1, of which 0 were waited for; matrix products, arithmetic and copies ran while one was open for 0% of the time, Pallas kernels for 28%

profile of v5, /device:TPU:0, one launch (start us, length us, event | category | flops | bytes accessed | tf_op | source)
XLA Modules:
  0.0 63.8 jit_solution(2556669627442974830)
XLA Ops:
  0.6 43.6 %expert_rows.1 = (bf16[512,1536]{1,0:T(8,128)(2,1)S(1)}, bf16[512,2560]{1,0:T(8,128)(2,1)S(1)}, bf16[512,2560]{1,0:T(8,128)(2,1)S(1)}, bf16[512,2560]{1,0:T(8,12...) custom-call(bf16[64,1536]{1,0:T(8,128)(2,1)} %u_hbm.1, ...), custom_call_target="tpu_custom_call" | custom-call | tf_op jit(solution)/shard_map/expert_rows/pallas_call | solution.py:401
  44.3 0.9 %collective-permute-start = (bf16[2,64,1536]{2,1,0:T(8,128)(2,1)S(1)}, bf16[2,64,1536]{2,1,0:T(8,128)(2,1)S(1)}, u32[]{:S(2)}, u32[]{:S(2)}) collective-permute-start(bf16[2,64,1536]{2,1,0:T(8,128)(2,1)S(1)} %get-tuple-element.19), channel_id=1, source_target_pairs={{0,6},{1,7},{2,4},{3,5},{4,2},{5,3},{6,0},{7,1}} | collective-permute-start | bytes 1179656 | tf_op jit(solution)/shard_map/ppermute | solution.py:431
  45.2 17.7 %weight_grads.1 = (f32[10,1536,256]{2,1,0:T(8,128)}, f32[10,1536,256]{2,1,0:T(8,128)}, f32[10,256,1536]{2,1,0:T(8,128)}, f32[40,1536]{1,0:T(8,128)}) custom-call(bf16[1536,512]{1,0:T(8,128)(2,1)S(1)} %get-tuple-element.20.xt, bf16[512,1536]{1,0:T(8,128)(2,1)S(1)} %get-tuple-element.21.dy, bf16[512,2560]{1,0:T(8,128)(2,1)S(1)} %get-tuple-element.22.ga, ...), custom_call_target="tpu_custom_call" | custom-call | flops 12079595520 | bytes 60293120 | tf_op jit(solution)/shard_map/weight_grads/pallas_call | solution.py:434
  62.9 0.0 collective-permute-done
  62.9 0.8 %fusion.1 = (bf16[64,1536]{1,0:T(8,128)(2,1)}, bf16[64,1536]{1,0:T(8,128)(2,1)}) fusion(f32[2,64,1536]{2,1,0:T(8,128)S(1)} %get-tuple-element.18, bf16[2,64,1536]{2,1,0:T(8,128)(2,1)S(1)} %collective-permute-done), kind=kLoop, calls=%fused_computation.3 | loop fusion | flops 589824 | bytes 1572864 | tf_op jit(solution)/shard_map/convert_element_type | solution.py:446
Async XLA Ops:
  44.3 18.7 %collective-permute-start = (bf16[2,64,1536]{2,1,0:T(8,128)(2,1)S(1)}, bf16[2,64,1536]{2,1,0:T(8,128)(2,1)S(1)}, u32[]{:S(2)}, u32[]{:S(2)}) collective-permute-start(bf16[2,64,1536]{2,1,0:T(8,128)(2,1)S(1)} %get-tuple-element.19), channel_id=1, source_target_pairs={{0,6},{1,7},{2,4},{3,5},{4,2},{5,3},{6,0},{7,1}} | collective-permute-start | bytes 1179656 | tf_op jit(solution)/shard_map/ppermute | solution.py:431

commit v6 on v5

--- a/solution.py
+++ b/solution.py
@@ -27,6 +27,10 @@
     return index + bit - 2 * index * bit
 
 
+def over_tokens(a, b):
+    return lax.dot_general(a, b, (((0,), (0,)), ((), ())), preferred_element_type=F32)
+
+
 def device_of(chip, other):
     ep, etp = lax.axis_index("ep"), lax.axis_index("etp")
     xb, yb = {OWN: (0, 0), DIAG: (1, 1), XN: (1, 0), YN: (0, 1)}[chip]
@@ -35,7 +39,7 @@
 
 def rows_kernel(
     sizes, u_hbm, dy_hbm, ids_hbm, wr_hbm, wg_hbm, wu_hbm, wd_hbm,
-    dy, ga, d1, d3, xt, dl_out, own_out, send_out,
+    dy, ga, d1, d3, xt, gu0, dn0, dl_out, own_out, send_out,
     u, ids_ref, wr_ref, rt, w1, w3, w2, sg, das, ys, yo, yr, xs, xr, dgacc, dgb, dgr, dlb, wr16,
     in_sem, w_sem, ag_send, ag_recv, small_send, small_recv, pair_send, pair_recv, xy_send, xy_recv,
 ):
@@ -307,6 +311,8 @@
     pair["od y"].start()
     send_xy("xy dx 1")
 
+    dn0[...] = over_tokens(ga[:, 0:ffn], dy[...])
+
     for c in dg_copies.values():
         c.wait_recv()
     dgate = dgb[0]
@@ -324,6 +330,7 @@
 
     sums_pass(0, (OWN, DIAG), 1, 0, steps, transpose=True)
     pair["od dx"].start()
+    gu0[...] = dot(xt[...], jnp.concatenate([d1[:, 0:ffn], d3[:, 0:ffn]], axis=1))
     du_router = dot(dlb[0], wr16[...])
     wait_recv(dl_copies.values())
     dl_out[...] = dlb[...].reshape(8 * tok, LANES)
@@ -341,43 +348,75 @@
             c.wait_send()
 
 
-def grads_kernel(sizes, xt, dy, ga, d1, d3, dl, dwg_hbm, dwu_hbm, dwd_hbm, dwr_ref, gu, dn, sems):
+def grads_kernel(sizes, xt, dy, ga, d1, d3, gu0, dn0, dl, dwg_hbm, dwu_hbm, dwd_hbm, dwr_ref, gu, dn, sems):
     local_exp, ffn = sizes
 
-    def copies(e, slot):
+    def copies(e, slot, wide=None, deep=None):
+        wide = gu.at[slot] if wide is None else wide
+        deep = dn.at[slot] if deep is None else deep
         return [
-            pltpu.make_async_copy(gu.at[slot, :, pl.ds(0, ffn)], dwg_hbm.at[e], sems.at[0, slot]),
-            pltpu.make_async_copy(gu.at[slot, :, pl.ds(ffn, ffn)], dwu_hbm.at[e], sems.at[1, slot]),
-            pltpu.make_async_copy(dn.at[slot], dwd_hbm.at[e], sems.at[2, slot]),
+            pltpu.make_async_copy(wide.at[:, pl.ds(0, ffn)], dwg_hbm.at[e], sems.at[0, slot]),
+            pltpu.make_async_copy(wide.at[:, pl.ds(ffn, ffn)], dwu_hbm.at[e], sems.at[1, slot]),
+            pltpu.make_async_copy(deep, dwd_hbm.at[e], sems.at[2, slot]),
         ]
 
-    def one(e, slot):
-        cols = pl.ds(pl.multiple_of(e * ffn, ffn), ffn)
-        gu[slot] = dot(xt[...], jnp.concatenate([d1[:, cols], d3[:, cols]], axis=1))
-        for c in copies(e, slot)[:2]:
+    def columns(e):
+        return pl.ds(pl.multiple_of(e * ffn, ffn), ffn)
+
+    def make_wide(e, slot):
+        gu[slot] = dot(xt[...], jnp.concatenate([d1[:, columns(e)], d3[:, columns(e)]], axis=1))
+
+    def make_deep(e, slot):
+        dn[slot] = over_tokens(ga[:, columns(e)], dy[...])
+
+    def start(e, slot, which=slice(0, 3)):
+        for c in copies(e, slot)[which]:
             c.start()
-        dn[slot] = lax.dot_general(ga[:, cols], dy[...], (((0,), (0,)), ((), ())), preferred_element_type=F32)
-        copies(e, slot)[2].start()
+
+    def wait(e, slot):
+        for c in copies(e, slot):
+            c.wait()
+
+    first = copies(0, 4, gu0, dn0)
+    for c in first:
+        c.start()
 
     def body(i, carry):
-        for slot in (0, 1):
-
-            @pl.when(i > 0)
-            def _():
-                for c in copies(2 * i + slot - 2, slot):
-                    c.wait()
-
-            one(2 * i + slot, slot)
+        e, slot = 1 + 2 * i, 2 * (i % 2)
+
+        @pl.when(i >= 2)
+        def _():
+            for k in (0, 1):
+                wait(e + k - 4, slot + k)
+
+        for k in (0, 1):
+            make_wide(e + k, slot + k)
+            make_deep(e + k, slot + k)
+        for k in (0, 1):
+            start(e + k, slot + k)
         return carry
 
-    lax.fori_loop(0, local_exp // 2, body, 0)
-    wide = dot_t(dl[...].T, xt[...])
-    wide = wide[0:64] + wide[64:128]
+    rounds = (local_exp - 1) // 2
+    lax.fori_loop(0, rounds, body, 0)
+    made = [(1 + 2 * i + k, 2 * (i % 2) + k) for i in range(rounds) for k in (0, 1)]
+    if local_exp % 2 == 0:
+        e, slot = local_exp - 1, 2 * (rounds % 2)
+        wait(e - 4, slot)
+        make_wide(e, slot)
+        start(e, slot, slice(0, 2))
+        make_deep(e, slot)
+        start(e, slot, slice(2, 3))
+        made = made[-3:] + [(e, slot)]
+    else:
+        made = made[-4:]
+    folded = dot_t(dl[...].T, xt[...])
+    folded = folded[0:64] + folded[64:128]
     for g in range(dwr_ref.shape[0] // local_exp):
-        dwr_ref[g * local_exp : (g + 1) * local_exp, :] = wide[g * GROUP : g * GROUP + local_exp]
-    for slot in (0, 1):
-        for c in copies(local_exp - 2 + slot, slot):
-            c.wait()
+        dwr_ref[g * local_exp : (g + 1) * local_exp, :] = folded[g * GROUP : g * GROUP + local_exp]
+    for e, slot in made:
+        wait(e, slot)
+    for c in first:
+        c.wait()
 
 
 def solution(mesh):
@@ -398,15 +437,15 @@
         vmem_spec = pl.BlockSpec(memory_space=pltpu.VMEM)
         S = jax.ShapeDtypeStruct
         dma = pltpu.SemaphoreType.DMA
-        dy, ga, d1, d3, xt, dl, own, send = pl.pallas_call(
+        dy, ga, d1, d3, xt, gu0, dn0, dl, own, send = pl.pallas_call(
             functools.partial(rows_kernel, (tok, d_model, ffn, local_exp, experts, top_k)),
             name="expert_rows",
             in_specs=[any_spec] * 7,
-            out_specs=[vmem_spec] * 8,
+            out_specs=[vmem_spec] * 10,
             out_shape=[
                 pltpu.VMEM((rows, d_model), BF16),
                 pltpu.VMEM((rows, wide), BF16), pltpu.VMEM((rows, wide), BF16), pltpu.VMEM((rows, wide), BF16),
-                pltpu.VMEM((d_model, rows), BF16), pltpu.VMEM((rows, LANES), BF16),
+                pltpu.VMEM((d_model, rows), BF16), pltpu.VMEM((d_model, 2 * ffn), F32), pltpu.VMEM((ffn, d_model), F32), pltpu.VMEM((rows, LANES), BF16),
                 pltpu.VMEM((2, tok, d_model), F32), pltpu.VMEM((2, tok, d_model), BF16),
             ],
             scratch_shapes=[
@@ -424,21 +463,21 @@
                 dma((4,)), dma((3, local_exp)), dma((3, 8)), dma((3, 8)), dma((16,)), dma((16,)),
                 dma((5,)), dma((5,)), dma((2, 3)), dma((2, 3)),
             ],
-            compiler_params=pltpu.CompilerParams(collective_id=0, has_side_effects=True, vmem_limit_bytes=48 * 1024 * 1024),
+            compiler_params=pltpu.CompilerParams(collective_id=0, has_side_effects=True, vmem_limit_bytes=43 * 1024 * 1024),
         )(u_loc, dy_loc, ids_loc.T, w_router.T, w_gate, w_up, w_down)
 
         n_ep, n_etp = lax.axis_size("ep"), lax.axis_size("etp")
         got = lax.ppermute(send, ("etp", "ep"), [(i, i ^ (n_ep + 2)) for i in range(n_ep * n_etp)])
 
-        kept = [pltpu.with_memory_space_constraint(a, pltpu.VMEM) for a in (xt, dy, ga, d1, d3, dl)]
+        kept = [pltpu.with_memory_space_constraint(a, pltpu.VMEM) for a in (xt, dy, ga, d1, d3, gu0, dn0, dl)]
         dwg, dwu, dwd, dwr = pl.pallas_call(
             functools.partial(grads_kernel, (local_exp, ffn)),
             name="weight_grads",
-            in_specs=[vmem_spec] * 6,
+            in_specs=[vmem_spec] * 8,
             out_specs=[any_spec] * 3 + [vmem_spec],
             out_shape=[S((local_exp, d_model, ffn), F32), S((local_exp, d_model, ffn), F32), S((local_exp, ffn, d_model), F32), S((experts, d_model), F32)],
-            scratch_shapes=[pltpu.VMEM((2, d_model, 2 * ffn), F32), pltpu.VMEM((2, ffn, d_model), F32), dma((3, 2))],
-            compiler_params=pltpu.CompilerParams(vmem_limit_bytes=24 * 1024 * 1024),
+            scratch_shapes=[pltpu.VMEM((4, d_model, 2 * ffn), F32), pltpu.VMEM((4, ffn, d_model), F32), dma((3, 5))],
+            compiler_params=pltpu.CompilerParams(vmem_limit_bytes=30 * 1024 * 1024),
             cost_estimate=pl.CostEstimate(flops=3 * 2 * rows * wide * d_model, bytes_accessed=12 * wide * d_model + 10 * rows * wide, transcendentals=0),
         )(*kept)
 

time: 63.9 us -> 63 us (0.986)
  Pallas kernels: 61.3 us -> 60.4 us
    pallas_call x1, Pallas kernels: 17.7 us -> 16.7 us  [device_step(): pl.pallas_call(functools.partial(grads_kernel, (local_exp, ffn)), name='w...]
  transfers between devices with their start and end apart: 1 -> 1, of which waited for: 0 -> 0; matrix products, arithmetic and copies ran while one was open for 0% -> 0% of each run, Pallas kernels for 28% -> 27%
where the time goes in v6:
time: 63 us; the launch traced here: 62.9 us
  Pallas kernels  60.4 us (96%)
  starting transfers between devices  1.08 us (2%)
  other arithmetic  0.81 us (1%)
  between operations  0.66 us (1%)
    pallas_call x1, Pallas kernels, device_step(): pl.pallas_call(functools.partial(rows_kernel, (tok, d_model, ffn, local_e...  43.7 us
    pallas_call x1, Pallas kernels, device_step(): pl.pallas_call(functools.partial(grads_kernel, (local_exp, ffn)), name='w...  16.7 us
  transfers between devices with their start and end apart: 1, of which 0 were waited for; matrix products, arithmetic and copies ran while one was open for 0% of the time, Pallas kernels for 27%

profile of v6, /device:TPU:0, one launch (start us, length us, event | category | flops | bytes accessed | tf_op | source)
XLA Modules:
  0.0 62.9 jit_solution(4186955346846584783)
XLA Ops:
  0.6 43.7 %expert_rows.1 = (bf16[512,1536]{1,0:T(8,128)(2,1)S(1)}, bf16[512,2560]{1,0:T(8,128)(2,1)S(1)}, bf16[512,2560]{1,0:T(8,128)(2,1)S(1)}, bf16[512,2560]{1,0:T(8,12...) custom-call(bf16[64,1536]{1,0:T(8,128)(2,1)} %u_hbm.1, ...), custom_call_target="tpu_custom_call" | custom-call | tf_op jit(solution)/shard_map/expert_rows/pallas_call | solution.py:440
  44.3 1.1 %collective-permute-start = (bf16[2,64,1536]{2,1,0:T(8,128)(2,1)S(1)}, bf16[2,64,1536]{2,1,0:T(8,128)(2,1)S(1)}, u32[]{:S(2)}, u32[]{:S(2)}) collective-permute-start(bf16[2,64,1536]{2,1,0:T(8,128)(2,1)S(1)} %get-tuple-element.21), channel_id=1, source_target_pairs={{0,6},{1,7},{2,4},{3,5},{4,2},{5,3},{6,0},{7,1}} | collective-permute-start | bytes 1179656 | tf_op jit(solution)/shard_map/ppermute | solution.py:470
  45.4 16.7 %weight_grads.1 = (f32[10,1536,256]{2,1,0:T(8,128)}, f32[10,1536,256]{2,1,0:T(8,128)}, f32[10,256,1536]{2,1,0:T(8,128)}, f32[40,1536]{1,0:T(8,128)}) custom-call(bf16[1536,512]{1,0:T(8,128)(2,1)S(1)} %get-tuple-element.22.xt, bf16[512,1536]{1,0:T(8,128)(2,1)S(1)} %get-tuple-element.23.dy, bf16[512,2560]{1,0:T(8,128)(2,1)S(1)} %get-tuple-element.24.ga, ...), custom_call_target="tpu_custom_call" | custom-call | flops 12079595520 | bytes 60293120 | tf_op jit(solution)/shard_map/weight_grads/pallas_call | solution.py:473
  62.1 0.0 collective-permute-done
  62.1 0.8 %fusion.1 = (bf16[64,1536]{1,0:T(8,128)(2,1)}, bf16[64,1536]{1,0:T(8,128)(2,1)}) fusion(f32[2,64,1536]{2,1,0:T(8,128)S(1)} %get-tuple-element.20, bf16[2,64,1536]{2,1,0:T(8,128)(2,1)S(1)} %collective-permute-done), kind=kLoop, calls=%fused_computation.3 | loop fusion | flops 589824 | bytes 1572864 | tf_op jit(solution)/shard_map/convert_element_type | solution.py:485
Async XLA Ops:
  44.3 17.8 %collective-permute-start = (bf16[2,64,1536]{2,1,0:T(8,128)(2,1)S(1)}, bf16[2,64,1536]{2,1,0:T(8,128)(2,1)S(1)}, u32[]{:S(2)}, u32[]{:S(2)}) collective-permute-start(bf16[2,64,1536]{2,1,0:T(8,128)(2,1)S(1)} %get-tuple-element.21), channel_id=1, source_target_pairs={{0,6},{1,7},{2,4},{3,5},{4,2},{5,3},{6,0},{7,1}} | collective-permute-start | bytes 1179656 | tf_op jit(solution)/shard_map/ppermute | solution.py:470

commit v7 on v6

--- a/solution.py
+++ b/solution.py
@@ -66,7 +66,7 @@
             for c in load_w(e)[which]:
                 c.start()
 
-    start_w(0, 1, slice(0, 2))
+    start_w(0, 3, slice(0, 2))
 
     barrier = pltpu.get_barrier_semaphore()
     others = [(chip, o) for chip in (OWN, DIAG, XN, YN) for o in (0, 1) if (chip, o) != (OWN, 0)]
@@ -111,7 +111,7 @@
     first_chips = (to_partner, to_chip[XN], to_chip[YN])
     for c in load_rows:
         c.wait()
-    start_w(1, local_exp, slice(0, 2))
+    start_w(3, local_exp, slice(0, 2))
     pl.semaphore_wait(barrier, len(others))
     send_part(1, first_chips)
 
@@ -152,16 +152,18 @@
         return jnp.sum(jnp.where(lanes == 64 + ep * GROUP + e, rt[rows, :], 0.0), axis=1, keepdims=True)
 
     def over_experts(lo, hi, one, which=None):
+        step = unroll if which is not None else hi - lo
+
         def body(i, carry):
             if which is not None:
-                for k in range(unroll):
-                    for c in load_w(i * unroll + k)[which]:
+                for k in range(step):
+                    for c in load_w(lo + i * step + k)[which]:
                         c.wait()
-            for k in range(unroll):
-                one(i * unroll + k, k % 2)
+            for k in range(step):
+                one(lo + i * step + k, k % 2)
             return carry
 
-        lax.fori_loop(lo // unroll, hi // unroll, body, 0)
+        lax.fori_loop(0, (hi - lo) // step, body, 0)
 
     def u_pass(row, count, lo, hi, first=False):
         rows = pl.ds(row, count)

time: 63 us -> 62.8 us (level)
  no operation moved by 1% of the time
where the time goes in v7:
time: 62.8 us; the launch traced here: 62.7 us
  Pallas kernels  59.9 us (95%)
  starting transfers between devices  1.3 us (2%)
  other arithmetic  0.81 us (1%)
  between operations  0.66 us (1%)
    pallas_call x1, Pallas kernels, device_step(): pl.pallas_call(functools.partial(rows_kernel, (tok, d_model, ffn, local_e...  43.3 us
    pallas_call x1, Pallas kernels, device_step(): pl.pallas_call(functools.partial(grads_kernel, (local_exp, ffn)), name='w...  16.7 us
    ppermute x1, starting transfers between devices, device_step(): lax.ppermute(send, ('etp', 'ep'), [(i, i ^ n_ep + 2) for i in range(n_ep...  1.3 us
  transfers between devices with their start and end apart: 1, of which 0 were waited for; matrix products, arithmetic and copies ran while one was open for 0% of the time, Pallas kernels for 27%

profile of v7, /device:TPU:0, one launch (start us, length us, event | category | flops | bytes accessed | tf_op | source)
XLA Modules:
  0.0 62.7 jit_solution(2179189892573654075)
XLA Ops:
  0.6 43.3 %expert_rows.1 = (bf16[512,1536]{1,0:T(8,128)(2,1)S(1)}, bf16[512,2560]{1,0:T(8,128)(2,1)S(1)}, bf16[512,2560]{1,0:T(8,128)(2,1)S(1)}, bf16[512,2560]{1,0:T(8,12...) custom-call(bf16[64,1536]{1,0:T(8,128)(2,1)} %u_hbm.1, ...), custom_call_target="tpu_custom_call" | custom-call | tf_op jit(solution)/shard_map/expert_rows/pallas_call | solution.py:442
  43.9 1.3 %collective-permute-start = (bf16[2,64,1536]{2,1,0:T(8,128)(2,1)S(1)}, bf16[2,64,1536]{2,1,0:T(8,128)(2,1)S(1)}, u32[]{:S(2)}, u32[]{:S(2)}) collective-permute-start(bf16[2,64,1536]{2,1,0:T(8,128)(2,1)S(1)} %get-tuple-element.21), channel_id=1, source_target_pairs={{0,6},{1,7},{2,4},{3,5},{4,2},{5,3},{6,0},{7,1}} | collective-permute-start | bytes 1179656 | tf_op jit(solution)/shard_map/ppermute | solution.py:472
  45.2 16.7 %weight_grads.1 = (f32[10,1536,256]{2,1,0:T(8,128)}, f32[10,1536,256]{2,1,0:T(8,128)}, f32[10,256,1536]{2,1,0:T(8,128)}, f32[40,1536]{1,0:T(8,128)}) custom-call(bf16[1536,512]{1,0:T(8,128)(2,1)S(1)} %get-tuple-element.22.xt, bf16[512,1536]{1,0:T(8,128)(2,1)S(1)} %get-tuple-element.23.dy, bf16[512,2560]{1,0:T(8,128)(2,1)S(1)} %get-tuple-element.24.ga, ...), custom_call_target="tpu_custom_call" | custom-call | flops 12079595520 | bytes 60293120 | tf_op jit(solution)/shard_map/weight_grads/pallas_call | solution.py:475
  61.9 0.0 collective-permute-done
  61.9 0.8 %fusion.1 = (bf16[64,1536]{1,0:T(8,128)(2,1)}, bf16[64,1536]{1,0:T(8,128)(2,1)}) fusion(f32[2,64,1536]{2,1,0:T(8,128)S(1)} %get-tuple-element.20, bf16[2,64,1536]{2,1,0:T(8,128)(2,1)S(1)} %collective-permute-done), kind=kLoop, calls=%fused_computation.3 | loop fusion | flops 589824 | bytes 1572864 | tf_op jit(solution)/shard_map/convert_element_type | solution.py:487
Async XLA Ops:
  43.9 18.0 %collective-permute-start = (bf16[2,64,1536]{2,1,0:T(8,128)(2,1)S(1)}, bf16[2,64,1536]{2,1,0:T(8,128)(2,1)S(1)}, u32[]{:S(2)}, u32[]{:S(2)}) collective-permute-start(bf16[2,64,1536]{2,1,0:T(8,128)(2,1)S(1)} %get-tuple-element.21), channel_id=1, source_target_pairs={{0,6},{1,7},{2,4},{3,5},{4,2},{5,3},{6,0},{7,1}} | collective-permute-start | bytes 1179656 | tf_op jit(solution)/shard_map/ppermute | solution.py:472
